TPU v7x, 128 devices: a whole 4x4x4 slice. The times are simulated.
128 devices in a mesh: col: 16 (over z, y), row: 8 (over x, core).
Axes of the slice: x: 4, y: 4, z: 4, core: 2. Of those that a mesh axis runs over, the one named last changes fastest.
Arguments:
- inter_mask: int32 [32768, 8192], P('row', 'col')
- emb_user: bfloat16 [32768, 64], P(('row', 'col'))
- emb_item: bfloat16 [8192, 64], P(('col', 'row'))
- triples: int32 [2048, 3], replicated
Outputs:
- output 1: bfloat16 [32768, 64], P(('row', 'col'))
- output 2: bfloat16 [8192, 64], P(('col', 'row'))
- output 3: float32 [2048], replicated
All inputs are finite; a program needn't handle non-finite values.
Results may differ from a plain program's by a relative error of at most 0.0065013.
Values are sent between devices in bfloat16 or wider.
A program may use at most 1 GiB of HBM per device.

v0:
```python
import jax
import jax.numpy as jnp
from jax import lax
from jax.sharding import PartitionSpec as P

LAYERS = 3


def solution(mesh):
    row_count = mesh.shape["row"]
    col_count = mesh.shape["col"]

    def lookup(emb_table, row_ids, row_start):
        local_ids = row_ids - row_start
        is_owned = (local_ids >= 0) & (local_ids < emb_table.shape[0])
        rows_got = jnp.take(emb_table, jnp.clip(local_ids, 0, emb_table.shape[0] - 1), axis=0).astype(jnp.float32)
        return jnp.where(is_owned[:, None], rows_got, 0.0)

    def device_body(mask_blk, user_shard, item_shard, triples):
        row_idx = lax.axis_index("row")
        col_idx = lax.axis_index("col")
        deg_user = lax.psum(jnp.sum(mask_blk, axis=1), "col")
        deg_item = lax.psum(jnp.sum(mask_blk, axis=0), "row")
        scale_user = lax.rsqrt(jnp.maximum(deg_user, 1).astype(jnp.float32))
        scale_item = lax.rsqrt(jnp.maximum(deg_item, 1).astype(jnp.float32))
        adj_norm = (mask_blk.astype(jnp.float32) * scale_user[:, None] * scale_item[None, :]).astype(jnp.bfloat16)
        cur_user = user_shard
        cur_item = item_shard
        total_user = user_shard.astype(jnp.float32)
        total_item = item_shard.astype(jnp.float32)
        for layer_idx in range(LAYERS):
            item_panel = lax.all_gather(cur_item, "row", axis=0, tiled=True)
            user_panel = lax.all_gather(cur_user, "col", axis=0, tiled=True)
            user_part = jnp.dot(adj_norm, item_panel, preferred_element_type=jnp.float32)
            item_part = jnp.einsum("ui,ud->id", adj_norm, user_panel, preferred_element_type=jnp.float32)
            cur_user = lax.psum_scatter(user_part, "col", scatter_dimension=0, tiled=True).astype(jnp.bfloat16)
            cur_item = lax.psum_scatter(item_part, "row", scatter_dimension=0, tiled=True).astype(jnp.bfloat16)
            total_user = total_user + cur_user.astype(jnp.float32)
            total_item = total_item + cur_item.astype(jnp.float32)
        out_user = (total_user / (LAYERS + 1)).astype(jnp.bfloat16)
        out_item = (total_item / (LAYERS + 1)).astype(jnp.bfloat16)
        user_start = (row_idx * col_count + col_idx) * out_user.shape[0]
        item_start = (col_idx * row_count + row_idx) * out_item.shape[0]
        picked = jnp.concatenate([
            lookup(out_user, triples[:, 0], user_start),
            lookup(out_item, triples[:, 1], item_start),
            lookup(out_item, triples[:, 2], item_start),
        ], axis=0)
        picked = lax.psum(picked, ("row", "col"))
        batch_n = triples.shape[0]
        vec_user = picked[:batch_n]
        vec_pos = picked[batch_n:2 * batch_n]
        vec_neg = picked[2 * batch_n:]
        margin = jnp.sum(vec_user * vec_pos, axis=1) - jnp.sum(vec_user * vec_neg, axis=1)
        bpr_loss = jax.nn.softplus(-margin)
        return out_user, out_item, bpr_loss

    return jax.shard_map(
        device_body,
        mesh=mesh,
        in_specs=(P("row", "col"), P(("row", "col"), None), P(("col", "row"), None), P()),
        out_specs=(P(("row", "col"), None), P(("col", "row"), None), P()),
        check_vma=False,
    )
```

profile of v0, /device:TPU:1, one launch (start us, length us, event | category | flops | bytes accessed | tf_op | source)
XLA Modules:
  0.0 638.0 jit_solution(9073068855081279712)
XLA Ops:
  7.2 4.1 fusion.4
  11.3 62.5 %psum.21 = s32[4096]{0:T(1024)S(1)} all-reduce(s32[4096]{0:T(1024)S(1)} %get-tuple-element.4), channel_id=1, replica_groups=mesh['col'=16,'row'=8] {'col'}, use_global_device_ids=true, to_apply=%region_1.0 | all-reduce | flops 4096 | bytes 32768 | tf_op jit(solution)/shard_map/psum | solution.py:22
  73.8 21.9 %psum.22 = s32[512]{0:T(512)S(1)} all-reduce(s32[512]{0:T(512)S(1)} %get-tuple-element.5), channel_id=1, replica_groups=mesh['col'=16,'row'=8] {'row'}, use_global_device_ids=true, to_apply=%region_3.0 | all-reduce | flops 512 | bytes 4096 | tf_op jit(solution)/shard_map/psum | solution.py:23
  95.7 17.2 %all_gather.19 = bf16[4096,64]{0,1:T(8,128)(2,1)S(1)} all-gather(bf16[256,64]{0,1:T(8,128)(2,1)S(1)} %copy-done.5), channel_id=1, replica_groups=mesh['col'=16,'row'=8] {'col'}, dimensions={0}, use_global_device_ids=true | all-gather | bytes 557056 | tf_op jit(solution)/shard_map/all_gather | solution.py:33
  112.9 4.0 multiply_convert_fusion
  117.0 1.9 copy-done.1
  118.9 2.0 fusion.6
  121.0 19.8 %all_gather.18 = bf16[512,64]{1,0:T(8,128)(2,1)S(1)} all-gather(bf16[64,64]{1,0:T(8,128)(2,1)S(1)} %copy-done.7), channel_id=1, replica_groups=mesh['col'=16,'row'=8] {'row'}, dimensions={0}, use_global_device_ids=true | all-gather | bytes 73728 | tf_op jit(solution)/shard_map/all_gather | solution.py:32
  140.7 4.6 fusion.5
  145.4 8.3 %reduce-scatter.9.cloned.1.call-done = f32[64,64]{1,0:T(8,128)} async-done(((f32[512,64]{1,0:T(8,128)}), f32[64,64]{1,0:T(8,128)}) %reduce-scatter.9.cloned.1.call-update) | async-done | bytes 16400 | tf_op jit(solution)/shard_map/reduce_scatter | solution.py:37
  154.4 15.5 %all_gather.20 = bf16[512,64]{1,0:T(8,128)(2,1)S(1)} all-gather(bf16[64,64]{1,0:T(8,128)(2,1)S(1)} %convert_element_type.76), channel_id=1, replica_groups=mesh['col'=16,'row'=8] {'row'}, dimensions={0}, use_global_device_ids=true | all-gather | bytes 73728 | tf_op jit(solution)/shard_map/all_gather | solution.py:32
  169.9 4.6 fusion.7
  174.6 55.9 %reduce-scatter.7.cloned.1.call-done = f32[256,64]{0,1:T(8,128)} async-done(((f32[4096,64]{0,1:T(8,128)}), f32[256,64]{0,1:T(8,128)}) %reduce-scatter.7.cloned.1.call-update) | async-done | bytes 65552 | tf_op jit(solution)/shard_map/reduce_scatter | solution.py:36
  231.3 19.0 %all_gather.21 = bf16[4096,64]{0,1:T(8,128)(2,1)S(1)} all-gather(bf16[256,64]{0,1:T(8,128)(2,1)S(1)} %convert_element_type.74), channel_id=1, replica_groups=mesh['col'=16,'row'=8] {'col'}, dimensions={0}, use_global_device_ids=true | all-gather | bytes 557056 | tf_op jit(solution)/shard_map/all_gather | solution.py:33
  250.3 4.2 fusion.8
  254.6 52.6 %reduce-scatter.11.cloned.1.call-done = f32[256,64]{0,1:T(8,128)} async-done(((f32[4096,64]{0,1:T(8,128)}), f32[256,64]{0,1:T(8,128)}) %reduce-scatter.11.cloned.1.call-update) | async-done | bytes 65552 | tf_op jit(solution)/shard_map/reduce_scatter | solution.py:36
  307.1 0.8 convert_element_type.77
  308.0 18.6 %all_gather.23 = bf16[4096,64]{0,1:T(8,128)(2,1)S(1)} all-gather(bf16[256,64]{0,1:T(8,128)(2,1)S(1)} %convert_element_type.77), channel_id=1, replica_groups=mesh['col'=16,'row'=8] {'col'}, dimensions={0}, use_global_device_ids=true | all-gather | bytes 557056 | tf_op jit(solution)/shard_map/all_gather | solution.py:33
  326.6 4.2 fusion.10
  330.9 7.9 %reduce-scatter.13.cloned.1.call-done = f32[64,64]{1,0:T(8,128)} async-done(((f32[512,64]{1,0:T(8,128)}), f32[64,64]{1,0:T(8,128)}) %reduce-scatter.13.cloned.1.call-update) | async-done | bytes 16400 | tf_op jit(solution)/shard_map/reduce_scatter | solution.py:37
  338.8 32.0 %reduce-scatter.17.cloned.1.call-done = f32[64,64]{1,0:T(8,128)} async-done(((f32[512,64]{1,0:T(8,128)}), f32[64,64]{1,0:T(8,128)}) %reduce-scatter.17.cloned.1.call-update) | async-done | bytes 16400 | tf_op jit(solution)/shard_map/reduce_scatter | solution.py:37
  371.6 15.8 %all_gather.22 = bf16[512,64]{1,0:T(8,128)(2,1)S(1)} all-gather(bf16[64,64]{1,0:T(8,128)(2,1)S(1)} %get-tuple-element.14), channel_id=1, replica_groups=mesh['col'=16,'row'=8] {'row'}, dimensions={0}, use_global_device_ids=true | all-gather | bytes 73728 | tf_op jit(solution)/shard_map/all_gather | solution.py:32
  387.3 4.6 fusion.9
  392.4 6.2 gather_fusion.2
  398.7 6.2 gather_fusion.1
  404.9 1.3 convert_select_fusion
  406.1 57.6 %reduce-scatter.15.cloned.1.call-done = f32[256,64]{0,1:T(8,128)} async-done(((f32[4096,64]{0,1:T(8,128)}), f32[256,64]{0,1:T(8,128)}) %reduce-scatter.15.cloned.1.call-update) | async-done | bytes 65552 | tf_op jit(solution)/shard_map/reduce_scatter | solution.py:36
  463.7 0.9 multiply_convert_fusion.1
  464.7 6.2 gather_fusion
  471.6 1.9 pad_maximum_fusion
  473.5 154.6 %all-reduce.2.cloned.1.call-done = f32[6144,64]{1,0:T(8,128)} async-done(((f32[6144,64]{1,0:T(8,128)}), f32[6144,64]{1,0:T(8,128)}) %all-reduce.2.cloned.1.call-update) | async-done | bytes 1572880 | tf_op jit(solution)/shard_map/psum | solution.py:49
  628.1 2.5 fusion
  (46 shorter events, 4.7 us)
Async XLA Ops:
  7.2 88.5 %copy-start.5 = (bf16[256,64]{0,1:T(8,128)(2,1)S(1)}, bf16[256,64]{0,1:T(8,128)(2,1)}, u32[]{:S(2)}) copy-start(bf16[256,64]{0,1:T(8,128)(2,1)} %param.7) | copy-start | bytes 98308
  7.2 146.5 %reduce-scatter.9.cloned.1.call-start = ((), (), s32[]{:S(2)}) async-start(), calls=%async_computation.7 | async-start | bytes 294912 | tf_op jit(solution)/shard_map/reduce_scatter | solution.py:37
  117.0 1.9 copy-start.1
  118.9 2.0 copy-start.7
  120.9 109.6 %reduce-scatter.7.cloned.1.call-start = ((), (), s32[]{:S(2)}) async-start(), calls=%async_computation.6 | async-start | bytes 1114112 | tf_op jit(solution)/shard_map/reduce_scatter | solution.py:36
  145.3 161.8 %reduce-scatter.11.cloned.1.call-start = ((), (), s32[]{:S(2)}) async-start(), calls=%async_computation.8 | async-start | bytes 1114112 | tf_op jit(solution)/shard_map/reduce_scatter | solution.py:36
  174.5 164.2 %reduce-scatter.13.cloned.1.call-start = ((), (), s32[]{:S(2)}) async-start(), calls=%async_computation.9 | async-start | bytes 294912 | tf_op jit(solution)/shard_map/reduce_scatter | solution.py:37
  254.5 116.3 %copy-start.4 = (f32[64,64]{1,0:T(8,128)S(1)}, f32[64,64]{1,0:T(8,128)}, u32[]{:S(2)}) copy-start(f32[64,64]{1,0:T(8,128)} %reduce-scatter.9.cloned.1.call-done) | copy-start | bytes 49156
  254.5 116.2 %reduce-scatter.17.cloned.1.call-start = ((), (), s32[]{:S(2)}) async-start(), calls=%async_computation.11 | async-start | bytes 294912 | tf_op jit(solution)/shard_map/reduce_scatter | solution.py:37
  330.8 132.9 %reduce-scatter.15.cloned.1.call-start = ((), (), s32[]{:S(2)}) async-start(), calls=%async_computation.10 | async-start | bytes 1114112 | tf_op jit(solution)/shard_map/reduce_scatter | solution.py:36
  371.5 27.1 %copy-start = (bf16[64,64]{1,0:T(8,128)(2,1)}, bf16[64,64]{1,0:T(8,128)(2,1)S(1)}, u32[]{:S(2)}) copy-start(bf16[64,64]{1,0:T(8,128)(2,1)S(1)} %get-tuple-element.13) | copy-start | bytes 24580
  387.3 4.8 copy-start.8
  391.9 236.2 %all-reduce.2.cloned.1.call-start = ((), (), s32[]{:S(2)}) async-start(), calls=%async_computation.12 | async-start | bytes 6291456 | tf_op jit(solution)/shard_map/psum | solution.py:49
  398.7 65.0 %copy-start.2 = (f32[256,64]{0,1:T(8,128)S(1)}, f32[256,64]{0,1:T(8,128)}, u32[]{:S(2)}) copy-start(f32[256,64]{0,1:T(8,128)} %reduce-scatter.7.cloned.1.call-done) | copy-start | bytes 196612
  398.7 65.0 %copy-start.3 = (f32[256,64]{0,1:T(8,128)S(1)}, f32[256,64]{0,1:T(8,128)}, u32[]{:S(2)}) copy-start(f32[256,64]{0,1:T(8,128)} %reduce-scatter.11.cloned.1.call-done) | copy-start | bytes 196612
  464.5 9.0 %copy-start.6 = (bf16[256,64]{0,1:T(8,128)(2,1)}, bf16[256,64]{0,1:T(8,128)(2,1)S(1)}, u32[]{:S(2)}) copy-start(bf16[256,64]{0,1:T(8,128)(2,1)S(1)} %multiply_convert_fusion.1) | copy-start | bytes 98308
Sparse Core Ops, SparseCore 0:
  121.0 32.6 reduce-scatter.8
  156.9 73.5 reduce-scatter.6
  233.7 73.3 reduce-scatter.10
  309.3 29.3 reduce-scatter.12
  341.0 29.7 reduce-scatter.16
  392.1 71.5 reduce-scatter.14
  473.7 154.3 all-reduce.1
where the time goes:
time: 639 us; the launch traced here: 638 us
  waiting for transfers between devices  369 us (58%)
  blocking collectives  190 us (30%)
  matrix products  24.1 us (4%)
  local copies, waits for them, and re-layouts  20.6 us (3%)
  other arithmetic  19.4 us (3%)
  between operations  14.3 us (2%)
    reduce_scatter x3, waiting for transfers between devices, device_body(): lax.psum_scatter(user_part, 'col', scatter_dimension=0, tiled=True)  166 us
    psum x1, waiting for transfers between devices, device_body(): picked = lax.psum(picked, ('row', 'col'))  155 us
    psum x1, blocking collectives, device_body(): deg_user = lax.psum(jnp.sum(mask_blk, axis=1), 'col')  62.5 us
    all_gather x3, blocking collectives, device_body(): user_panel = lax.all_gather(cur_user, 'col', axis=0, tiled=True)  54.8 us
    all_gather x3, blocking collectives, device_body(): item_panel = lax.all_gather(cur_item, 'row', axis=0, tiled=True)  51.1 us
    reduce_scatter x3, waiting for transfers between devices, device_body(): lax.psum_scatter(item_part, 'row', scatter_dimension=0, tiled=True)  48.1 us
    psum x1, blocking collectives, device_body(): deg_item = lax.psum(jnp.sum(mask_blk, axis=0), 'row')  21.9 us
    gather x3, local copies, waits for them, and re-layouts, lookup(): jnp.take(emb_table, jnp.clip(local_ids, 0, emb_table.shape[0] - 1), axis=0)  18.6 us
  transfers between devices with their start and end apart: 7, of which 7 were waited for; matrix products, arithmetic and copies ran while one was open for 5% of the time, Pallas kernels for 0%

commit v1 on v0

v1 whole, which is shorter than its diff:
```python
import functools

import jax
import jax.numpy as jnp
from jax import lax
from jax.experimental import pallas as pl
from jax.experimental.pallas import tpu as pltpu
from jax.sharding import PartitionSpec as P

LAYERS = 3
SIDE = 4
F32 = jnp.float32
BF16 = jnp.bfloat16
NN = (((1,), (0,)), ((), ()))
NT = (((1,), (1,)), ((), ()))
TN = (((0,), (0,)), ((), ()))


def mm(lhs, rhs, dims=NN):
    return lax.dot_general(lhs, rhs, dims, preferred_element_type=F32)


def identity(size):
    at_row = lax.broadcasted_iota(jnp.int32, (size, size), 0)
    at_col = lax.broadcasted_iota(jnp.int32, (size, size), 1)
    return jnp.where(at_row == at_col, 1.0, 0.0).astype(BF16)


def kernel(
    rows, mask_hbm, eu_ref, ei_ref, tri_ref, ou_ref, oi_ref, loss_ref,
    mask_buf, adj, ua, ub, pa, pb, ra, rb, sa, sb, qa, qb, utot,
    i_nat, i_pan, pi, ri, itot, du_own, du_y, du_ysum, du_z, di_own, di_got,
    picks, sc_own, sc_row, sc_rsum, sc_y, sc_ysum, sc_z, oi_nat,
    load_sem, send_sem, recv_sem,
):
    r = lax.axis_index("row")
    c = lax.axis_index("col")
    z, y = lax.div(c, SIDE), lax.rem(c, SIDE)
    half = ua.shape[-2]
    emb = 2 * half
    ublk = ua.shape[-1]
    chunks = SIDE * SIDE
    iblk = adj.shape[-1]
    isub = i_nat.shape[1]
    tiles = sc_own.shape[0]
    tw = sc_own.shape[1]

    def plus(base, k, n):
        return lax.rem(base + k, n)

    def y_dev(k):
        return {"col": z * SIDE + plus(y, k, SIDE)}

    def z_dev(k):
        return {"col": plus(z, k, SIDE) * SIDE + y}

    def r_dev(k):
        return {"row": plus(r, k, rows)}

    sides = (2, 1, 3)
    ring = tuple(range(1, rows))
    count = [0]
    sent = []

    def sems(n):
        first = count[0]
        count[0] += n
        return first

    def copy(src, dst, sem, dev):
        return pltpu.make_async_remote_copy(
            src_ref=src, dst_ref=dst, send_sem=send_sem.at[sem], recv_sem=recv_sem.at[sem],
            device_id=dev, device_id_type=pl.DeviceIdType.MESH)

    def push(sem, src, dst, dev):
        one = copy(src, dst, sem, dev)
        one.start()
        sent.append(one)

    def arrive(sem, dst, dev):
        copy(dst, dst, sem, dev).wait_recv()

    loads = [pltpu.make_async_copy(mask_hbm.at[pl.ds(j * ublk, ublk)], mask_buf.at[j], load_sem.at[j]) for j in range(chunks)]
    for one in loads:
        one.start()

    barrier = pltpu.get_barrier_semaphore()
    for k in (1, 2, 3):
        pl.semaphore_signal(barrier, inc=1, device_id=y_dev(k), device_id_type=pl.DeviceIdType.MESH)
        pl.semaphore_signal(barrier, inc=1, device_id=z_dev(k), device_id_type=pl.DeviceIdType.MESH)
    for k in ring:
        pl.semaphore_signal(barrier, inc=1, device_id=r_dev(k), device_id_type=pl.DeviceIdType.MESH)

    eye = identity(emb)
    user0 = mm(eye, eu_ref[...], NT)
    utot[...] = user0
    user0 = user0.astype(BF16)
    ua[0, y, z] = user0[:half]
    ub[0, z, y] = user0[half:]
    i_nat[r] = ei_ref[...]
    pl.semaphore_wait(barrier, 6 + len(ring))

    ug = [sems(4 * SIDE) for _ in range(LAYERS + 1)]

    def user_gather_1(l):
        for k in sides:
            push(ug[l] + k, ua.at[l, y, z], ua.at[l, y, z], z_dev(k))
            push(ug[l] + SIDE + k, ub.at[l, z, y], ub.at[l, z, y], y_dev(k))

    def user_gather_2(l):
        for k in (1, 3, 2):
            arrive(ug[l] + k, ua.at[l, y, plus(z, SIDE - k, SIDE)], z_dev(SIDE - k))
            arrive(ug[l] + SIDE + k, ub.at[l, z, plus(y, SIDE - k, SIDE)], y_dev(SIDE - k))
        for k in sides:
            push(ug[l] + 2 * SIDE + k, ua.at[l, y], ua.at[l, y], y_dev(k))
            push(ug[l] + 3 * SIDE + k, ub.at[l, z], ub.at[l, z], z_dev(k))

    def user_gather_end(l):
        for k in (1, 3, 2):
            arrive(ug[l] + 2 * SIDE + k, ua.at[l, plus(y, SIDE - k, SIDE)], y_dev(SIDE - k))
            arrive(ug[l] + 3 * SIDE + k, ub.at[l, plus(z, SIDE - k, SIDE)], z_dev(SIDE - k))

    us = [sems(4 * SIDE) for _ in range(LAYERS)]

    def user_product(l, panel):
        def step(j, carry):
            part = mm(panel, adj[j], NT)
            jz, jy = lax.div(j, SIDE), lax.rem(j, SIDE)
            pa[l, jy, jz] = part[:half]
            pb[l, jz, jy] = part[half:]
            return carry
        lax.fori_loop(0, chunks, step, 0, unroll=4)
        for k in sides:
            push(us[l] + k, pa.at[l, plus(y, k, SIDE)], ra.at[l, k - 1], y_dev(k))
            push(us[l] + SIDE + k, pb.at[l, plus(z, k, SIDE)], rb.at[l, k - 1], z_dev(k))

    def user_sum_1(l):
        for k in (1, 3, 2):
            arrive(us[l] + k, ra.at[l, k - 1], y_dev(SIDE - k))
            arrive(us[l] + SIDE + k, rb.at[l, k - 1], z_dev(SIDE - k))
        for j in range(SIDE):
            sa[l, j] = pa[l, y, j] + ra[l, 0, j] + ra[l, 1, j] + ra[l, 2, j]
            sb[l, j] = pb[l, z, j] + rb[l, 0, j] + rb[l, 1, j] + rb[l, 2, j]
        for k in sides:
            push(us[l] + 2 * SIDE + k, sa.at[l, plus(z, k, SIDE)], qa.at[l, k - 1], z_dev(k))
            push(us[l] + 3 * SIDE + k, sb.at[l, plus(y, k, SIDE)], qb.at[l, k - 1], y_dev(k))

    def user_sum_2(l):
        for k in (1, 3, 2):
            arrive(us[l] + 2 * SIDE + k, qa.at[l, k - 1], z_dev(SIDE - k))
            arrive(us[l] + 3 * SIDE + k, qb.at[l, k - 1], y_dev(SIDE - k))
        next_a = (sa[l, z] + qa[l, 0] + qa[l, 1] + qa[l, 2]).astype(BF16)
        next_b = (sb[l, y] + qb[l, 0] + qb[l, 1] + qb[l, 2]).astype(BF16)
        utot[pl.ds(0, half)] += next_a.astype(F32)
        utot[pl.ds(half, half)] += next_b.astype(F32)
        return next_a, next_b

    def user_keep(l, next_a, next_b):
        ua[l, y, z] = next_a
        ub[l, z, y] = next_b

    ig = [sems(rows) for _ in range(LAYERS + 1)]
    isum = [sems(rows) for _ in range(LAYERS)]

    def item_product(l):
        def step(j, acc):
            jz, jy = lax.div(j, SIDE), lax.rem(j, SIDE)
            lhs = jnp.concatenate([ua[l, jy, jz], ub[l, jz, jy]], axis=0)
            return acc + mm(lhs, adj[j])
        acc = lax.fori_loop(0, chunks, step, jnp.zeros((emb, iblk), F32), unroll=4)
        pi[l] = acc.reshape(pi.shape[1:])
        for k in ring:
            push(isum[l] + k, pi.at[l, plus(r, k, rows)], ri.at[l, k - 1], r_dev(k))

    def item_gather(l, mine):
        i_pan[l, r] = mine
        for k in ring:
            push(ig[l] + k, i_pan.at[l, r], i_pan.at[l, r], r_dev(k))

    def item_sum(l):
        for k in ring:
            arrive(isum[l] + k, ri.at[l, k - 1], r_dev(rows - k))
        acc = pi[l, r]
        for k in ring:
            acc = acc + ri[l, k - 1]
        mine = acc.astype(BF16).astype(F32)
        itot[...] += mine
        return mine

    def item_panel(l):
        for k in ring:
            arrive(ig[l] + k, i_pan.at[l, plus(r, rows - k, rows)], r_dev(rows - k))
        return i_pan[l].reshape(emb, iblk).astype(BF16)

    user_gather_1(0)
    for k in ring:
        push(ig[0] + k, i_nat.at[r], i_nat.at[r], r_dev(k))

    du_s, dz_s, di_s = sems(SIDE), sems(SIDE), sems(rows)
    ones = jnp.ones((8, iblk), BF16)
    di_acc = jnp.zeros((8, iblk), jnp.int32)
    for j in range(chunks):
        loads[j].wait()
        blk = mask_buf[j]
        di_acc = di_acc + jnp.sum(blk.reshape(ublk // 8, 8, iblk), axis=0)
        blk = blk.astype(F32).astype(BF16)
        adj[j] = blk
        du_own[pl.ds(j, 1), :] = mm(ones, blk, NT)[:1]
    di_own[...] = di_acc.astype(F32)
    for k in sides:
        push(du_s + k, du_own, du_y.at[k - 1], y_dev(k))
    for k in ring:
        push(di_s + k, di_own, di_got.at[k - 1], r_dev(k))
    user_gather_2(0)
    for k in ring:
        arrive(ig[0] + k, i_nat.at[plus(r, rows - k, rows)], r_dev(rows - k))
    item0 = mm(eye, i_nat[...].reshape(iblk, emb), NT)
    i_pan[0] = item0.reshape(i_pan.shape[1:])
    itot[...] = i_pan[0, r]
    item0 = item0.astype(BF16)
    for k in (1, 3, 2):
        arrive(du_s + k, du_y.at[k - 1], y_dev(SIDE - k))
    du_ysum[...] = du_own[...] + du_y[0] + du_y[1] + du_y[2]
    for k in sides:
        push(dz_s + k, du_ysum, du_z.at[k - 1], z_dev(k))
    for k in ring:
        arrive(di_s + k, di_got.at[k - 1], r_dev(rows - k))
    deg_i = di_own[...]
    for k in ring:
        deg_i = deg_i + di_got[k - 1]
    deg_i = jnp.sum(deg_i, axis=0, keepdims=True)
    scale_i = lax.rsqrt(jnp.maximum(deg_i, 1.0))
    for k in (1, 3, 2):
        arrive(dz_s + k, du_z.at[k - 1], z_dev(SIDE - k))
    deg_u = du_ysum[...] + du_z[0] + du_z[1] + du_z[2]
    scale_u = lax.rsqrt(jnp.maximum(deg_u, 1.0)).T
    for j in range(chunks):
        adj[j] = (adj[j].astype(F32) * scale_u[:, j:j + 1] * scale_i).astype(BF16)

    user_product(0, item0)
    user_gather_end(0)
    item_product(0)
    item_gather(1, item_sum(0))
    user_sum_1(0)
    user_product(1, item_panel(1))
    user_keep(1, *user_sum_2(0))
    user_gather_1(1)
    user_sum_1(1)
    user_gather_2(1)
    user_keep(2, *user_sum_2(1))
    user_gather_1(2)
    user_gather_end(1)
    item_product(1)
    user_gather_2(2)
    item_gather(2, item_sum(1))
    user_product(2, item_panel(2))
    user_gather_end(2)
    item_product(2)
    item_sum(2)
    item_gather(3, (itot[...] / (LAYERS + 1)).astype(BF16).astype(F32))
    user_sum_1(2)

    out_it = item_panel(3)
    oi_nat[...] = mm(out_it, eye, TN).reshape(oi_nat.shape)
    oi_ref[...] = oi_nat[r].astype(BF16)
    lane = ublk
    at_row = lax.broadcasted_iota(jnp.int32, (lane, tw), 0)

    def pick_items(which, t):
        local = tri_ref[which, pl.ds(t, 1), :] - c * iblk
        got = jnp.zeros((emb, tw), F32)
        for h in range(iblk // lane):
            hit = jnp.where(local - h * lane == at_row, 1.0, 0.0).astype(BF16)
            got = got + mm(out_it[:, h * lane:(h + 1) * lane], hit)
        return got

    for t in range(tiles):
        picks[0, t] = pick_items(1, t)
        picks[1, t] = pick_items(2, t)

    user_sum_2(2)
    out_ut = (utot[...] / (LAYERS + 1)).astype(BF16)
    ua[3, y, z] = out_ut[:half]
    ub[3, z, y] = out_ut[half:]
    user_gather_1(3)
    ou_ref[...] = mm(out_ut, eye, TN).astype(BF16)
    user_gather_2(3)
    user_gather_end(3)

    stack_a = ua[3].reshape(chunks * half, ublk)
    stack_b = ub[3].reshape(chunks * half, ublk)
    for t in range(tiles):
        local = tri_ref[0, pl.ds(t, 1), :] - r * (chunks * ublk)
        blk_id = lax.div(local, ublk)
        blk_id = jnp.where(local < 0, -1, blk_id)
        hit = jnp.where(local - blk_id * ublk == at_row, 1.0, 0.0).astype(BF16)
        got_a = mm(stack_a, hit)
        got_b = mm(stack_b, hit)
        vec_a = jnp.zeros((half, tw), F32)
        vec_b = jnp.zeros((half, tw), F32)
        for jz in range(SIDE):
            for jy in range(SIDE):
                here = blk_id == jz * SIDE + jy
                ja = (jy * SIDE + jz) * half
                jb = (jz * SIDE + jy) * half
                vec_a = vec_a + jnp.where(here, got_a[ja:ja + half], 0.0)
                vec_b = vec_b + jnp.where(here, got_b[jb:jb + half], 0.0)
        vec = jnp.concatenate([vec_a, vec_b], axis=0)
        pos = jnp.sum(vec * picks[0, t], axis=0, keepdims=True)
        neg = jnp.sum(vec * picks[1, t], axis=0, keepdims=True)
        sc_own[pl.ds(t, 1), :] = pos - neg

    s_r, s_y, s_z = sems(rows), sems(SIDE), sems(SIDE)
    for k in ring:
        push(s_r + k, sc_own, sc_row.at[k - 1], r_dev(k))
    for k in ring:
        arrive(s_r + k, sc_row.at[k - 1], r_dev(rows - k))
    acc = sc_own[...]
    for k in ring:
        acc = acc + sc_row[k - 1]
    sc_rsum[...] = acc
    for k in sides:
        push(s_y + k, sc_rsum, sc_y.at[k - 1], y_dev(k))
    for k in sides:
        arrive(s_y + k, sc_y.at[k - 1], y_dev(SIDE - k))
    sc_ysum[...] = sc_rsum[...] + (sc_y[0] + sc_y[1] + sc_y[2])
    for k in sides:
        push(s_z + k, sc_ysum, sc_z.at[k - 1], z_dev(k))
    for k in sides:
        arrive(s_z + k, sc_z.at[k - 1], z_dev(SIDE - k))
    neg_x = -(sc_ysum[...] + (sc_z[0] + sc_z[1] + sc_z[2]))
    loss_ref[...] = jnp.maximum(neg_x, 0.0) + jnp.log1p(jnp.exp(-jnp.abs(neg_x)))
    for one in sent:
        one.wait_send()
    assert count[0] <= send_sem.shape[0]


def solution(mesh):
    rows = mesh.shape["row"]
    cols = mesh.shape["col"]

    def device_body(mask_blk, user_shard, item_shard, triples):
        ublk, emb = user_shard.shape
        isub = item_shard.shape[0]
        iblk = mask_blk.shape[1]
        batch = triples.shape[0]
        half = emb // 2
        width = emb // rows
        tw = 256
        tiles = batch // tw
        tri = triples.T.reshape(3, tiles, tw)
        n_sem = (2 * LAYERS + 1) * 16 + rows * (2 * LAYERS + 1) + 2 * SIDE + rows + rows + 2 * SIDE
        vmem = pltpu.VMEM
        out_user, out_item, loss = pl.pallas_call(
            functools.partial(kernel, rows),
            name="lightgcn",
            out_shape=(
                jax.ShapeDtypeStruct((ublk, emb), BF16),
                jax.ShapeDtypeStruct((isub, emb), BF16),
                jax.ShapeDtypeStruct((tiles, tw), F32),
            ),
            in_specs=[pl.BlockSpec(memory_space=pl.ANY)] + [pl.BlockSpec(memory_space=vmem)] * 3,
            out_specs=tuple([pl.BlockSpec(memory_space=vmem)] * 3),
            scratch_shapes=[
                vmem((cols, ublk, iblk), jnp.int32),
                vmem((cols, ublk, iblk), BF16),
                vmem((LAYERS + 1, SIDE, SIDE, half, ublk), BF16),
                vmem((LAYERS + 1, SIDE, SIDE, half, ublk), BF16),
                vmem((LAYERS, SIDE, SIDE, half, ublk), F32),
                vmem((LAYERS, SIDE, SIDE, half, ublk), F32),
                vmem((LAYERS, 3, SIDE, half, ublk), F32),
                vmem((LAYERS, 3, SIDE, half, ublk), F32),
                vmem((LAYERS, SIDE, half, ublk), F32),
                vmem((LAYERS, SIDE, half, ublk), F32),
                vmem((LAYERS, 3, half, ublk), F32),
                vmem((LAYERS, 3, half, ublk), F32),
                vmem((emb, ublk), F32),
                vmem((rows, isub, emb), BF16),
                vmem((LAYERS + 1, rows, width, iblk), F32),
                vmem((LAYERS, rows, width, iblk), F32),
                vmem((LAYERS, rows - 1, width, iblk), F32),
                vmem((width, iblk), F32),
                vmem((cols, ublk), F32),
                vmem((3, cols, ublk), F32),
                vmem((cols, ublk), F32),
                vmem((3, cols, ublk), F32),
                vmem((8, iblk), F32),
                vmem((rows - 1, 8, iblk), F32),
                vmem((2, tiles, emb, tw), F32),
                vmem((tiles, tw), F32),
                vmem((rows - 1, tiles, tw), F32),
                vmem((tiles, tw), F32),
                vmem((3, tiles, tw), F32),
                vmem((tiles, tw), F32),
                vmem((3, tiles, tw), F32),
                vmem((rows, isub, emb), F32),
                pltpu.SemaphoreType.DMA((cols,)),
                pltpu.SemaphoreType.DMA((n_sem,)),
                pltpu.SemaphoreType.DMA((n_sem,)),
            ],
            compiler_params=pltpu.CompilerParams(collective_id=0, has_side_effects=True),
        )(mask_blk, user_shard, item_shard, tri)
        return out_user, out_item, loss.reshape(batch)

    return jax.shard_map(
        device_body,
        mesh=mesh,
        in_specs=(P("row", "col"), P(("row", "col"), None), P(("col", "row"), None), P()),
        out_specs=(P(("row", "col"), None), P(("col", "row"), None), P()),
        check_vma=False,
    )
```

time: 639 us -> 104 us (0.16)
  waiting for transfers between devices: 369 us -> 0 us
  blocking collectives: 190 us -> 0 us
  Pallas kernels: 0 us -> 94.8 us
  matrix products: 24.1 us -> 0 us
  other arithmetic: 19.4 us -> 0 us
  between operations: 14.3 us -> 0.64 us
  local copies, waits for them, and re-layouts: 20.6 us -> 7.01 us
    reduce_scatter x6 -> x0, waiting for transfers between devices: 214 us -> none  [the longest x3 166 us: device_body(): lax.psum_scatter(user_part, 'col', scatter_dimension=0, tiled=True)]
    psum x1 -> x0, waiting for transfers between devices: 155 us -> none  [device_body(): picked = lax.psum(picked, ('row', 'col'))]
    all_gather x6 -> x0, blocking collectives: 106 us -> none  [the longest x3 54.8 us: device_body(): user_panel = lax.all_gather(cur_user, 'col', axis=0, tiled=True)]
    pallas_call x0 -> x1, Pallas kernels: none -> 94.8 us  [device_body(): pl.pallas_call(functools.partial(kernel, rows), name='lightgcn', out_shap...]
    psum x2 -> x0, blocking collectives: 84.4 us -> none  [the longest x1 62.5 us: device_body(): deg_user = lax.psum(jnp.sum(mask_blk, axis=1), 'col')]
    dot_general x6 -> x0, matrix products: 24.1 us -> none  [the longest x3 13.7 us: device_body(): jnp.dot(adj_norm, item_panel, preferred_element_type=jnp.float32)]
    gather x3 -> x0, local copies, waits for them, and re-layouts: 18.6 us -> none  [lookup(): jnp.take(emb_table, jnp.clip(local_ids, 0, emb_table.shape[0] - 1), axis=0)]
    convert_element_type x6 -> x0, other arithmetic: 8.12 us -> none  [the longest x1 4.03 us: device_body(): (mask_blk.astype(jnp.float32) * scale_user[:, None] * scale_item[None, :]...]
  transfers between devices with their start and end apart: 7 -> 0, of which waited for: 7 -> 0; matrix products, arithmetic and copies ran while one was open for 5% -> 0% of each run, Pallas kernels for 0% -> 0%
where the time goes in v1:
time: 104 us; the launch traced here: 102 us
  Pallas kernels  94.8 us (91%)
  local copies, waits for them, and re-layouts  7.01 us (7%)
    pallas_call x1, Pallas kernels, device_body(): pl.pallas_call(functools.partial(kernel, rows), name='lightgcn', out_shap...  94.8 us
    unnamed x5, local copies, waits for them, and re-layouts  7.01 us

profile of v1, /device:TPU:1, one launch (start us, length us, event | category | flops | bytes accessed | tf_op | source)
XLA Modules:
  0.0 102.4 jit_solution(3413937478345958629)
XLA Ops:
  0.6 1.4 %copy.12 = s32[1,3,8,256]{3,2,1,0:T(8,128)} copy(s32[1,3,8,256]{3,1,2,0:T(4,128)} %bitcast.8) | data formatting | bytes 49152
  2.0 1.5 %copy.7.eu_ref = bf16[256,64]{1,0:T(8,128)(2,1)} copy(bf16[256,64]{0,1:T(8,128)(2,1)} %param.5) | data formatting | bytes 65536 | tf_op args[1]
  3.5 94.8 %lightgcn.1 = (bf16[256,64]{1,0:T(8,128)(2,1)}, bf16[64,64]{1,0:T(8,128)(2,1)}, f32[8,256]{1,0:T(8,128)}) custom-call(s32[4096,512]{1,0:T(8,128)} %mask_hbm.1, bf16[256,64]{1,0:T(8,128)(2,1)} %copy.7.eu_ref, bf16[64,64]{1,0:T(8,128)(2,1)} %ei_ref.1, s32[3,8,256]{2,1,0:T(8,128)} %bitcast.7), custom_call_target="tpu_custom_call" | custom-call | tf_op jit(solution)/shard_map/lightgcn/pallas_call | solution.py:354
  98.3 1.5 %copy.8 = bf16[256,64]{0,1:T(8,128)(2,1)} copy(bf16[256,64]{1,0:T(8,128)(2,1)} %get-tuple-element.9) | data formatting | bytes 65536
  99.8 1.3 %copy.10 = f32[1,2,8,128]{3,1,2,0:T(2,128)} copy(f32[1,2,8,128]{3,2,1,0:T(8,128)} %bitcast.10) | data formatting | bytes 16384
  101.1 1.3 %copy.14 = bf16[64,64]{1,0:T(8,128)(2,1)} copy(bf16[64,64]{1,0:T(8,128)(2,1)} %get-tuple-element.16) | data formatting | bytes 16384

commit v2 on v1

--- a/solution.py
+++ b/solution.py
@@ -30,7 +30,7 @@
     rows, mask_hbm, eu_ref, ei_ref, tri_ref, ou_ref, oi_ref, loss_ref,
     mask_buf, adj, ua, ub, pa, pb, ra, rb, sa, sb, qa, qb, utot,
     i_nat, i_pan, pi, ri, itot, du_own, du_y, du_ysum, du_z, di_own, di_got,
-    picks, sc_own, sc_row, sc_rsum, sc_y, sc_ysum, sc_z, oi_nat,
+    picks, sc_own, sc_row, sc_sum, sc_col, oi_nat,
     load_sem, send_sem, recv_sem,
 ):
     r = lax.axis_index("row")
@@ -42,8 +42,7 @@
     chunks = SIDE * SIDE
     iblk = adj.shape[-1]
     isub = i_nat.shape[1]
-    tiles = sc_own.shape[0]
-    tw = sc_own.shape[1]
+    tiles, tw = picks.shape[1], picks.shape[3]
 
     def plus(base, k, n):
         return lax.rem(base + k, n)
@@ -57,7 +56,11 @@
     def r_dev(k):
         return {"row": plus(r, k, rows)}
 
+    def c_dev(k):
+        return {"col": plus(c, k, chunks)}
+
     sides = (2, 1, 3)
+    plane = tuple(range(1, chunks))
     ring = tuple(range(1, rows))
     count = [0]
     sent = []
@@ -85,72 +88,83 @@
         one.start()
 
     barrier = pltpu.get_barrier_semaphore()
-    for k in (1, 2, 3):
-        pl.semaphore_signal(barrier, inc=1, device_id=y_dev(k), device_id_type=pl.DeviceIdType.MESH)
-        pl.semaphore_signal(barrier, inc=1, device_id=z_dev(k), device_id_type=pl.DeviceIdType.MESH)
+    for k in plane:
+        pl.semaphore_signal(barrier, inc=1, device_id=c_dev(k), device_id_type=pl.DeviceIdType.MESH)
     for k in ring:
         pl.semaphore_signal(barrier, inc=1, device_id=r_dev(k), device_id_type=pl.DeviceIdType.MESH)
 
     eye = identity(emb)
-    user0 = mm(eye, eu_ref[...], NT)
-    utot[...] = user0
-    user0 = user0.astype(BF16)
+    user0 = eu_ref[...]
+    utot[...] = user0.astype(F32)
     ua[0, y, z] = user0[:half]
     ub[0, z, y] = user0[half:]
     i_nat[r] = ei_ref[...]
-    pl.semaphore_wait(barrier, 6 + len(ring))
-
-    ug = [sems(4 * SIDE) for _ in range(LAYERS + 1)]
-
-    def user_gather_1(l):
+    pl.semaphore_wait(barrier, len(plane) + len(ring))
+
+    ug = [sems(10 * SIDE) for _ in range(LAYERS + 1)]
+
+    def user_gather_start(l):
         for k in sides:
             push(ug[l] + k, ua.at[l, y, z], ua.at[l, y, z], z_dev(k))
-            push(ug[l] + SIDE + k, ub.at[l, z, y], ub.at[l, z, y], y_dev(k))
-
-    def user_gather_2(l):
-        for k in (1, 3, 2):
-            arrive(ug[l] + k, ua.at[l, y, plus(z, SIDE - k, SIDE)], z_dev(SIDE - k))
-            arrive(ug[l] + SIDE + k, ub.at[l, z, plus(y, SIDE - k, SIDE)], y_dev(SIDE - k))
+            push(ug[l] + 4 + k, ub.at[l, z, y], ub.at[l, z, y], y_dev(k))
         for k in sides:
-            push(ug[l] + 2 * SIDE + k, ua.at[l, y], ua.at[l, y], y_dev(k))
-            push(ug[l] + 3 * SIDE + k, ub.at[l, z], ub.at[l, z], z_dev(k))
+            push(ug[l] + 8 + k, ua.at[l, y, z], ua.at[l, y, z], y_dev(k))
+            push(ug[l] + 12 + k, ub.at[l, z, y], ub.at[l, z, y], z_dev(k))
+
+    def user_gather_fwd(l):
+        for q in (1, 3, 2):
+            at_z, at_y = plus(z, SIDE - q, SIDE), plus(y, SIDE - q, SIDE)
+            arrive(ug[l] + q, ua.at[l, y, at_z], z_dev(SIDE - q))
+            arrive(ug[l] + 4 + q, ub.at[l, z, at_y], y_dev(SIDE - q))
+            for k in sides:
+                push(ug[l] + 8 + 8 * q + k, ua.at[l, y, at_z], ua.at[l, y, at_z], y_dev(k))
+                push(ug[l] + 12 + 8 * q + k, ub.at[l, z, at_y], ub.at[l, z, at_y], z_dev(k))
 
     def user_gather_end(l):
-        for k in (1, 3, 2):
-            arrive(ug[l] + 2 * SIDE + k, ua.at[l, plus(y, SIDE - k, SIDE)], y_dev(SIDE - k))
-            arrive(ug[l] + 3 * SIDE + k, ub.at[l, plus(z, SIDE - k, SIDE)], z_dev(SIDE - k))
-
-    us = [sems(4 * SIDE) for _ in range(LAYERS)]
+        for q in (0, 1, 3, 2):
+            for k in (1, 3, 2):
+                at_z, at_y = plus(z, SIDE - q, SIDE), plus(y, SIDE - q, SIDE)
+                from_z, from_y = plus(z, SIDE - k, SIDE), plus(y, SIDE - k, SIDE)
+                arrive(ug[l] + 8 + 8 * q + k, ua.at[l, from_y, at_z], y_dev(SIDE - k))
+                arrive(ug[l] + 12 + 8 * q + k, ub.at[l, from_z, at_y], z_dev(SIDE - k))
+
+    us = [sems(8 * SIDE) for _ in range(LAYERS)]
+    groups = ((2, 2), (1, 1), (0, 1))
 
     def user_product(l, panel):
         def step(j, carry):
             part = mm(panel, adj[j], NT)
             jz, jy = lax.div(j, SIDE), lax.rem(j, SIDE)
-            pa[l, jy, jz] = part[:half]
-            pb[l, jz, jy] = part[half:]
+            pa[l, jy, plus(jz + SIDE, -z, SIDE)] = part[:half]
+            pb[l, jz, plus(jy + SIDE, -y, SIDE)] = part[half:]
             return carry
         lax.fori_loop(0, chunks, step, 0, unroll=4)
-        for k in sides:
-            push(us[l] + k, pa.at[l, plus(y, k, SIDE)], ra.at[l, k - 1], y_dev(k))
-            push(us[l] + SIDE + k, pb.at[l, plus(z, k, SIDE)], rb.at[l, k - 1], z_dev(k))
+        for g, (lo, n) in enumerate(groups):
+            for k in sides:
+                part = pl.ds(lo, n)
+                push(us[l] + 8 * g + k, pa.at[l, plus(y, k, SIDE), part], ra.at[l, k - 1, part], y_dev(k))
+                push(us[l] + 8 * g + 4 + k, pb.at[l, plus(z, k, SIDE), part], rb.at[l, k - 1, part], z_dev(k))
 
     def user_sum_1(l):
-        for k in (1, 3, 2):
-            arrive(us[l] + k, ra.at[l, k - 1], y_dev(SIDE - k))
-            arrive(us[l] + SIDE + k, rb.at[l, k - 1], z_dev(SIDE - k))
-        for j in range(SIDE):
-            sa[l, j] = pa[l, y, j] + ra[l, 0, j] + ra[l, 1, j] + ra[l, 2, j]
-            sb[l, j] = pb[l, z, j] + rb[l, 0, j] + rb[l, 1, j] + rb[l, 2, j]
-        for k in sides:
-            push(us[l] + 2 * SIDE + k, sa.at[l, plus(z, k, SIDE)], qa.at[l, k - 1], z_dev(k))
-            push(us[l] + 3 * SIDE + k, sb.at[l, plus(y, k, SIDE)], qb.at[l, k - 1], y_dev(k))
+        for g, (lo, n) in enumerate(groups):
+            part = pl.ds(lo, n)
+            for k in (1, 3, 2):
+                arrive(us[l] + 8 * g + k, ra.at[l, k - 1, part], y_dev(SIDE - k))
+                arrive(us[l] + 8 * g + 4 + k, rb.at[l, k - 1, part], z_dev(SIDE - k))
+            for j in range(lo, lo + n):
+                sa[l, j] = pa[l, y, j] + ra[l, 0, j] + ra[l, 1, j] + ra[l, 2, j]
+                sb[l, j] = pb[l, z, j] + rb[l, 0, j] + rb[l, 1, j] + rb[l, 2, j]
+            for k in range(lo, lo + n):
+                if k:
+                    push(us[l] + 24 + k, sa.at[l, k], qa.at[l, k - 1], z_dev(k))
+                    push(us[l] + 28 + k, sb.at[l, k], qb.at[l, k - 1], y_dev(k))
 
     def user_sum_2(l):
-        for k in (1, 3, 2):
-            arrive(us[l] + 2 * SIDE + k, qa.at[l, k - 1], z_dev(SIDE - k))
-            arrive(us[l] + 3 * SIDE + k, qb.at[l, k - 1], y_dev(SIDE - k))
-        next_a = (sa[l, z] + qa[l, 0] + qa[l, 1] + qa[l, 2]).astype(BF16)
-        next_b = (sb[l, y] + qb[l, 0] + qb[l, 1] + qb[l, 2]).astype(BF16)
+        for k in (2, 3, 1):
+            arrive(us[l] + 24 + k, qa.at[l, k - 1], z_dev(SIDE - k))
+            arrive(us[l] + 28 + k, qb.at[l, k - 1], y_dev(SIDE - k))
+        next_a = (sa[l, 0] + qa[l, 0] + qa[l, 1] + qa[l, 2]).astype(BF16)
+        next_b = (sb[l, 0] + qb[l, 0] + qb[l, 1] + qb[l, 2]).astype(BF16)
         utot[pl.ds(0, half)] += next_a.astype(F32)
         utot[pl.ds(half, half)] += next_b.astype(F32)
         return next_a, next_b
@@ -192,7 +206,7 @@
             arrive(ig[l] + k, i_pan.at[l, plus(r, rows - k, rows)], r_dev(rows - k))
         return i_pan[l].reshape(emb, iblk).astype(BF16)
 
-    user_gather_1(0)
+    user_gather_start(0)
     for k in ring:
         push(ig[0] + k, i_nat.at[r], i_nat.at[r], r_dev(k))
 
@@ -211,7 +225,7 @@
         push(du_s + k, du_own, du_y.at[k - 1], y_dev(k))
     for k in ring:
         push(di_s + k, di_own, di_got.at[k - 1], r_dev(k))
-    user_gather_2(0)
+    user_gather_fwd(0)
     for k in ring:
         arrive(ig[0] + k, i_nat.at[plus(r, rows - k, rows)], r_dev(rows - k))
     item0 = mm(eye, i_nat[...].reshape(iblk, emb), NT)
@@ -235,30 +249,36 @@
     deg_u = du_ysum[...] + du_z[0] + du_z[1] + du_z[2]
     scale_u = lax.rsqrt(jnp.maximum(deg_u, 1.0)).T
     for j in range(chunks):
-        adj[j] = (adj[j].astype(F32) * scale_u[:, j:j + 1] * scale_i).astype(BF16)
+        adj[j] = adj[j] * (scale_u[:, j:j + 1] * scale_i).astype(BF16)
 
     user_product(0, item0)
     user_gather_end(0)
     item_product(0)
     item_gather(1, item_sum(0))
     user_sum_1(0)
+    user_keep(1, *user_sum_2(0))
+    user_gather_start(1)
+    user_gather_fwd(1)
     user_product(1, item_panel(1))
-    user_keep(1, *user_sum_2(0))
-    user_gather_1(1)
-    user_sum_1(1)
-    user_gather_2(1)
-    user_keep(2, *user_sum_2(1))
-    user_gather_1(2)
     user_gather_end(1)
     item_product(1)
-    user_gather_2(2)
     item_gather(2, item_sum(1))
+    user_sum_1(1)
+    user_keep(2, *user_sum_2(1))
+    user_gather_start(2)
     user_product(2, item_panel(2))
+    user_gather_fwd(2)
+    user_sum_1(2)
     user_gather_end(2)
     item_product(2)
+    user_sum_2(2)
+    out_ut = (utot[...] / (LAYERS + 1)).astype(BF16)
+    user_keep(3, out_ut[:half], out_ut[half:])
+    user_gather_start(3)
     item_sum(2)
     item_gather(3, (itot[...] / (LAYERS + 1)).astype(BF16).astype(F32))
-    user_sum_1(2)
+    ou_ref[...] = out_ut
+    user_gather_fwd(3)
 
     out_it = item_panel(3)
     oi_nat[...] = mm(out_it, eye, TN).reshape(oi_nat.shape)
@@ -267,7 +287,7 @@
     at_row = lax.broadcasted_iota(jnp.int32, (lane, tw), 0)
 
     def pick_items(which, t):
-        local = tri_ref[which, pl.ds(t, 1), :] - c * iblk
+        local = tri_ref[which:which + 1, t * tw:(t + 1) * tw] - c * iblk
         got = jnp.zeros((emb, tw), F32)
         for h in range(iblk // lane):
             hit = jnp.where(local - h * lane == at_row, 1.0, 0.0).astype(BF16)
@@ -278,19 +298,11 @@
         picks[0, t] = pick_items(1, t)
         picks[1, t] = pick_items(2, t)
 
-    user_sum_2(2)
-    out_ut = (utot[...] / (LAYERS + 1)).astype(BF16)
-    ua[3, y, z] = out_ut[:half]
-    ub[3, z, y] = out_ut[half:]
-    user_gather_1(3)
-    ou_ref[...] = mm(out_ut, eye, TN).astype(BF16)
-    user_gather_2(3)
     user_gather_end(3)
-
     stack_a = ua[3].reshape(chunks * half, ublk)
     stack_b = ub[3].reshape(chunks * half, ublk)
     for t in range(tiles):
-        local = tri_ref[0, pl.ds(t, 1), :] - r * (chunks * ublk)
+        local = tri_ref[0:1, t * tw:(t + 1) * tw] - r * (chunks * ublk)
         blk_id = lax.div(local, ublk)
         blk_id = jnp.where(local < 0, -1, blk_id)
         hit = jnp.where(local - blk_id * ublk == at_row, 1.0, 0.0).astype(BF16)
@@ -308,9 +320,10 @@
         vec = jnp.concatenate([vec_a, vec_b], axis=0)
         pos = jnp.sum(vec * picks[0, t], axis=0, keepdims=True)
         neg = jnp.sum(vec * picks[1, t], axis=0, keepdims=True)
-        sc_own[pl.ds(t, 1), :] = pos - neg
-
-    s_r, s_y, s_z = sems(rows), sems(SIDE), sems(SIDE)
+        for h in range(tw // 128):
+            sc_own[pl.ds(t * (tw // 128) + h, 1), :] = (pos - neg)[:, h * 128:(h + 1) * 128]
+
+    s_r, s_c = sems(rows), sems(chunks)
     for k in ring:
         push(s_r + k, sc_own, sc_row.at[k - 1], r_dev(k))
     for k in ring:
@@ -318,21 +331,24 @@
     acc = sc_own[...]
     for k in ring:
         acc = acc + sc_row[k - 1]
-    sc_rsum[...] = acc
-    for k in sides:
-        push(s_y + k, sc_rsum, sc_y.at[k - 1], y_dev(k))
-    for k in sides:
-        arrive(s_y + k, sc_y.at[k - 1], y_dev(SIDE - k))
-    sc_ysum[...] = sc_rsum[...] + (sc_y[0] + sc_y[1] + sc_y[2])
-    for k in sides:
-        push(s_z + k, sc_ysum, sc_z.at[k - 1], z_dev(k))
-    for k in sides:
-        arrive(s_z + k, sc_z.at[k - 1], z_dev(SIDE - k))
-    neg_x = -(sc_ysum[...] + (sc_z[0] + sc_z[1] + sc_z[2]))
+    sc_sum[...] = acc
+    for k in plane:
+        push(s_c + k, sc_sum, sc_col.at[k - 1], c_dev(k))
+    for k in plane:
+        arrive(s_c + k, sc_col.at[k - 1], c_dev(chunks - k))
+    for k in plane:
+        acc = acc + sc_col[k - 1]
+    neg_x = -acc
     loss_ref[...] = jnp.maximum(neg_x, 0.0) + jnp.log1p(jnp.exp(-jnp.abs(neg_x)))
     for one in sent:
         one.wait_send()
     assert count[0] <= send_sem.shape[0]
+
+
+def emit(ou_in, oi_in, loss_in, ou_ref, oi_ref, loss_ref):
+    ou_ref[...] = ou_in[...]
+    oi_ref[...] = oi_in[...]
+    loss_ref[...] = loss_in[...]
 
 
 def solution(mesh):
@@ -348,16 +364,15 @@
         width = emb // rows
         tw = 256
         tiles = batch // tw
-        tri = triples.T.reshape(3, tiles, tw)
-        n_sem = (2 * LAYERS + 1) * 16 + rows * (2 * LAYERS + 1) + 2 * SIDE + rows + rows + 2 * SIDE
+        n_sem = 40 * (LAYERS + 1) + 32 * LAYERS + rows * (2 * LAYERS + 1) + 2 * SIDE + rows + rows + cols
         vmem = pltpu.VMEM
         out_user, out_item, loss = pl.pallas_call(
             functools.partial(kernel, rows),
             name="lightgcn",
             out_shape=(
-                jax.ShapeDtypeStruct((ublk, emb), BF16),
+                jax.ShapeDtypeStruct((emb, ublk), BF16),
                 jax.ShapeDtypeStruct((isub, emb), BF16),
-                jax.ShapeDtypeStruct((tiles, tw), F32),
+                jax.ShapeDtypeStruct((batch // 128, 128), F32),
             ),
             in_specs=[pl.BlockSpec(memory_space=pl.ANY)] + [pl.BlockSpec(memory_space=vmem)] * 3,
             out_specs=tuple([pl.BlockSpec(memory_space=vmem)] * 3),
@@ -387,20 +402,27 @@
                 vmem((8, iblk), F32),
                 vmem((rows - 1, 8, iblk), F32),
                 vmem((2, tiles, emb, tw), F32),
-                vmem((tiles, tw), F32),
-                vmem((rows - 1, tiles, tw), F32),
-                vmem((tiles, tw), F32),
-                vmem((3, tiles, tw), F32),
-                vmem((tiles, tw), F32),
-                vmem((3, tiles, tw), F32),
+                vmem((batch // 128, 128), F32),
+                vmem((rows - 1, batch // 128, 128), F32),
+                vmem((batch // 128, 128), F32),
+                vmem((cols - 1, batch // 128, 128), F32),
                 vmem((rows, isub, emb), F32),
                 pltpu.SemaphoreType.DMA((cols,)),
                 pltpu.SemaphoreType.DMA((n_sem,)),
                 pltpu.SemaphoreType.DMA((n_sem,)),
             ],
             compiler_params=pltpu.CompilerParams(collective_id=0, has_side_effects=True),
-        )(mask_blk, user_shard, item_shard, tri)
-        return out_user, out_item, loss.reshape(batch)
+        )(mask_blk, user_shard.T, item_shard, triples.T)
+        out_user, out_item, loss = pl.pallas_call(
+            emit,
+            name="emit",
+            out_shape=(
+                jax.ShapeDtypeStruct((emb, ublk), BF16),
+                jax.ShapeDtypeStruct((isub, emb), BF16),
+                jax.ShapeDtypeStruct((batch // 128, 128), F32),
+            ),
+        )(out_user, out_item, loss)
+        return out_user.T, out_item, loss.reshape(batch)
 
     return jax.shard_map(
         device_body,

time: 104 us -> 92.3 us (0.89); the launches traced: 102 us -> 92 us
  local copies, waits for them, and re-layouts: 7.01 us -> 0 us
  Pallas kernels: 94.8 us -> 91.4 us
    unnamed x5 -> x0, local copies, waits for them, and re-layouts: 7.01 us -> none
    pallas_call x1, Pallas kernels: 94.8 us -> 90 us  [device_body(): pl.pallas_call(functools.partial(kernel, rows), name='lightgcn', out_shap...]
    pallas_call x0 -> x1, Pallas kernels: none -> 1.4 us  [device_body(): pl.pallas_call(emit, name='emit', out_shape=(jax.ShapeDtypeStruct((emb, u...]
where the time goes in v2:
time: 92.3 us; the launch traced here: 92 us
  Pallas kernels  91.4 us (99%)
    pallas_call x1, Pallas kernels, device_body(): pl.pallas_call(functools.partial(kernel, rows), name='lightgcn', out_shap...  90 us

profile of v2, /device:TPU:1, one launch (start us, length us, event | category | flops | bytes accessed | tf_op | source)
XLA Modules:
  0.0 92.0 jit_solution(6647864160839087358)
XLA Ops:
  0.6 90.0 %lightgcn.1 = (bf16[64,256]{1,0:T(8,128)(2,1)}, bf16[64,64]{1,0:T(8,128)(2,1)}, f32[16,128]{1,0:T(8,128)}) custom-call(s32[4096,512]{1,0:T(8,128)} %mask_hbm.1, bf16[64,256]{1,0:T(8,128)(2,1)} %bitcast.4, bf16[64,64]{1,0:T(8,128)(2,1)} %ei_ref.1, s32[3,2048]{1,0:T(4,128)} %bitcast.5), custom_call_target="tpu_custom_call" | custom-call | tf_op jit(solution)/shard_map/lightgcn/pallas_call | solution.py:369
  90.6 1.4 %emit.1 = (bf16[64,256]{1,0:T(8,128)(2,1)}, bf16[64,64]{1,0:T(8,128)(2,1)}, f32[16,128]{1,0:T(8,128)}) custom-call(bf16[64,256]{1,0:T(8,128)(2,1)} %get-tuple-element.9.ou_in, bf16[64,64]{1,0:T(8,128)(2,1)} %get-tuple-element.10.oi_in, f32[16,128]{1,0:T(8,128)} %get-tuple-element.11.loss_in), custom_call_target="tpu_custom_call" | custom-call | tf_op jit(solution)/shard_map/emit/pallas_call | solution.py:416

commit v3 on v2

--- a/solution.py
+++ b/solution.py
@@ -1,4 +1,5 @@
 import functools
+import math
 
 import jax
 import jax.numpy as jnp
@@ -70,18 +71,17 @@
         count[0] += n
         return first
 
-    def copy(src, dst, sem, dev):
+    def copy(src, dst, sem, dev, out=0):
         return pltpu.make_async_remote_copy(
-            src_ref=src, dst_ref=dst, send_sem=send_sem.at[sem], recv_sem=recv_sem.at[sem],
+            src_ref=src, dst_ref=dst, send_sem=send_sem.at[out], recv_sem=recv_sem.at[sem],
             device_id=dev, device_id_type=pl.DeviceIdType.MESH)
 
     def push(sem, src, dst, dev):
-        one = copy(src, dst, sem, dev)
-        one.start()
-        sent.append(one)
-
-    def arrive(sem, dst, dev):
-        copy(dst, dst, sem, dev).wait_recv()
+        copy(src, dst, sem, dev).start()
+        sent.append(math.prod(src.shape) * src.dtype.itemsize)
+
+    def arrive(sem, whole):
+        copy(whole, whole, sem, {"row": r}).wait_recv()
 
     loads = [pltpu.make_async_copy(mask_hbm.at[pl.ds(j * ublk, ublk)], mask_buf.at[j], load_sem.at[j]) for j in range(chunks)]
     for one in loads:
@@ -101,34 +101,31 @@
     i_nat[r] = ei_ref[...]
     pl.semaphore_wait(barrier, len(plane) + len(ring))
 
-    ug = [sems(10 * SIDE) for _ in range(LAYERS + 1)]
+    ug = [sems(10) for _ in range(LAYERS + 1)]
 
     def user_gather_start(l):
         for k in sides:
             push(ug[l] + k, ua.at[l, y, z], ua.at[l, y, z], z_dev(k))
             push(ug[l] + 4 + k, ub.at[l, z, y], ub.at[l, z, y], y_dev(k))
         for k in sides:
-            push(ug[l] + 8 + k, ua.at[l, y, z], ua.at[l, y, z], y_dev(k))
-            push(ug[l] + 12 + k, ub.at[l, z, y], ub.at[l, z, y], z_dev(k))
+            push(ug[l] + 8, ua.at[l, y, z], ua.at[l, y, z], y_dev(k))
+            push(ug[l] + 9, ub.at[l, z, y], ub.at[l, z, y], z_dev(k))
 
     def user_gather_fwd(l):
         for q in (1, 3, 2):
             at_z, at_y = plus(z, SIDE - q, SIDE), plus(y, SIDE - q, SIDE)
-            arrive(ug[l] + q, ua.at[l, y, at_z], z_dev(SIDE - q))
-            arrive(ug[l] + 4 + q, ub.at[l, z, at_y], y_dev(SIDE - q))
+            arrive(ug[l] + q, ua.at[l, y, at_z])
             for k in sides:
-                push(ug[l] + 8 + 8 * q + k, ua.at[l, y, at_z], ua.at[l, y, at_z], y_dev(k))
-                push(ug[l] + 12 + 8 * q + k, ub.at[l, z, at_y], ub.at[l, z, at_y], z_dev(k))
+                push(ug[l] + 8, ua.at[l, y, at_z], ua.at[l, y, at_z], y_dev(k))
+            arrive(ug[l] + 4 + q, ub.at[l, z, at_y])
+            for k in sides:
+                push(ug[l] + 9, ub.at[l, z, at_y], ub.at[l, z, at_y], z_dev(k))
 
     def user_gather_end(l):
-        for q in (0, 1, 3, 2):
-            for k in (1, 3, 2):
-                at_z, at_y = plus(z, SIDE - q, SIDE), plus(y, SIDE - q, SIDE)
-                from_z, from_y = plus(z, SIDE - k, SIDE), plus(y, SIDE - k, SIDE)
-                arrive(ug[l] + 8 + 8 * q + k, ua.at[l, from_y, at_z], y_dev(SIDE - k))
-                arrive(ug[l] + 12 + 8 * q + k, ub.at[l, from_z, at_y], z_dev(SIDE - k))
-
-    us = [sems(8 * SIDE) for _ in range(LAYERS)]
+        arrive(ug[l] + 8, ua.at[l, pl.ds(0, SIDE - 1)])
+        arrive(ug[l] + 9, ub.at[l, pl.ds(0, SIDE - 1)])
+
+    us = [sems(8) for _ in range(LAYERS)]
     groups = ((2, 2), (1, 1), (0, 1))
 
     def user_product(l, panel):
@@ -142,27 +139,25 @@
         for g, (lo, n) in enumerate(groups):
             for k in sides:
                 part = pl.ds(lo, n)
-                push(us[l] + 8 * g + k, pa.at[l, plus(y, k, SIDE), part], ra.at[l, k - 1, part], y_dev(k))
-                push(us[l] + 8 * g + 4 + k, pb.at[l, plus(z, k, SIDE), part], rb.at[l, k - 1, part], z_dev(k))
+                push(us[l] + g, pa.at[l, plus(y, k, SIDE), part], ra.at[l, k - 1, part], y_dev(k))
+                push(us[l] + 4 + g, pb.at[l, plus(z, k, SIDE), part], rb.at[l, k - 1, part], z_dev(k))
 
     def user_sum_1(l):
         for g, (lo, n) in enumerate(groups):
             part = pl.ds(lo, n)
-            for k in (1, 3, 2):
-                arrive(us[l] + 8 * g + k, ra.at[l, k - 1, part], y_dev(SIDE - k))
-                arrive(us[l] + 8 * g + 4 + k, rb.at[l, k - 1, part], z_dev(SIDE - k))
+            arrive(us[l] + g, ra.at[l, :, part])
+            arrive(us[l] + 4 + g, rb.at[l, :, part])
             for j in range(lo, lo + n):
                 sa[l, j] = pa[l, y, j] + ra[l, 0, j] + ra[l, 1, j] + ra[l, 2, j]
                 sb[l, j] = pb[l, z, j] + rb[l, 0, j] + rb[l, 1, j] + rb[l, 2, j]
             for k in range(lo, lo + n):
                 if k:
-                    push(us[l] + 24 + k, sa.at[l, k], qa.at[l, k - 1], z_dev(k))
-                    push(us[l] + 28 + k, sb.at[l, k], qb.at[l, k - 1], y_dev(k))
+                    push(us[l] + 3, sa.at[l, k], qa.at[l, k - 1], z_dev(k))
+                    push(us[l] + 7, sb.at[l, k], qb.at[l, k - 1], y_dev(k))
 
     def user_sum_2(l):
-        for k in (2, 3, 1):
-            arrive(us[l] + 24 + k, qa.at[l, k - 1], z_dev(SIDE - k))
-            arrive(us[l] + 28 + k, qb.at[l, k - 1], y_dev(SIDE - k))
+        arrive(us[l] + 3, qa.at[l])
+        arrive(us[l] + 7, qb.at[l])
         next_a = (sa[l, 0] + qa[l, 0] + qa[l, 1] + qa[l, 2]).astype(BF16)
         next_b = (sb[l, 0] + qb[l, 0] + qb[l, 1] + qb[l, 2]).astype(BF16)
         utot[pl.ds(0, half)] += next_a.astype(F32)
@@ -173,8 +168,8 @@
         ua[l, y, z] = next_a
         ub[l, z, y] = next_b
 
-    ig = [sems(rows) for _ in range(LAYERS + 1)]
-    isum = [sems(rows) for _ in range(LAYERS)]
+    ig = [sems(1) for _ in range(LAYERS + 1)]
+    isum = [sems(1) for _ in range(LAYERS)]
 
     def item_product(l):
         def step(j, acc):
@@ -184,16 +179,15 @@
         acc = lax.fori_loop(0, chunks, step, jnp.zeros((emb, iblk), F32), unroll=4)
         pi[l] = acc.reshape(pi.shape[1:])
         for k in ring:
-            push(isum[l] + k, pi.at[l, plus(r, k, rows)], ri.at[l, k - 1], r_dev(k))
+            push(isum[l], pi.at[l, plus(r, k, rows)], ri.at[l, k - 1], r_dev(k))
 
     def item_gather(l, mine):
         i_pan[l, r] = mine
         for k in ring:
-            push(ig[l] + k, i_pan.at[l, r], i_pan.at[l, r], r_dev(k))
+            push(ig[l], i_pan.at[l, r], i_pan.at[l, r], r_dev(k))
 
     def item_sum(l):
-        for k in ring:
-            arrive(isum[l] + k, ri.at[l, k - 1], r_dev(rows - k))
+        arrive(isum[l], ri.at[l])
         acc = pi[l, r]
         for k in ring:
             acc = acc + ri[l, k - 1]
@@ -202,15 +196,14 @@
         return mine
 
     def item_panel(l):
-        for k in ring:
-            arrive(ig[l] + k, i_pan.at[l, plus(r, rows - k, rows)], r_dev(rows - k))
+        arrive(ig[l], i_pan.at[l, pl.ds(0, rows - 1)])
         return i_pan[l].reshape(emb, iblk).astype(BF16)
 
     user_gather_start(0)
     for k in ring:
-        push(ig[0] + k, i_nat.at[r], i_nat.at[r], r_dev(k))
-
-    du_s, dz_s, di_s = sems(SIDE), sems(SIDE), sems(rows)
+        copy(i_nat.at[r], i_nat.at[r], ig[0], r_dev(k), 1).start()
+
+    du_s, dz_s, di_s = sems(1), sems(1), sems(1)
     ones = jnp.ones((8, iblk), BF16)
     di_acc = jnp.zeros((8, iblk), jnp.int32)
     for j in range(chunks):
@@ -222,30 +215,26 @@
         du_own[pl.ds(j, 1), :] = mm(ones, blk, NT)[:1]
     di_own[...] = di_acc.astype(F32)
     for k in sides:
-        push(du_s + k, du_own, du_y.at[k - 1], y_dev(k))
-    for k in ring:
-        push(di_s + k, di_own, di_got.at[k - 1], r_dev(k))
+        push(du_s, du_own, du_y.at[k - 1], y_dev(k))
+    for k in ring:
+        push(di_s, di_own, di_got.at[k - 1], r_dev(k))
     user_gather_fwd(0)
-    for k in ring:
-        arrive(ig[0] + k, i_nat.at[plus(r, rows - k, rows)], r_dev(rows - k))
+    arrive(ig[0], i_nat.at[pl.ds(0, rows - 1)])
     item0 = mm(eye, i_nat[...].reshape(iblk, emb), NT)
     i_pan[0] = item0.reshape(i_pan.shape[1:])
     itot[...] = i_pan[0, r]
     item0 = item0.astype(BF16)
-    for k in (1, 3, 2):
-        arrive(du_s + k, du_y.at[k - 1], y_dev(SIDE - k))
+    arrive(du_s, du_y)
     du_ysum[...] = du_own[...] + du_y[0] + du_y[1] + du_y[2]
     for k in sides:
-        push(dz_s + k, du_ysum, du_z.at[k - 1], z_dev(k))
-    for k in ring:
-        arrive(di_s + k, di_got.at[k - 1], r_dev(rows - k))
+        push(dz_s, du_ysum, du_z.at[k - 1], z_dev(k))
+    arrive(di_s, di_got)
     deg_i = di_own[...]
     for k in ring:
         deg_i = deg_i + di_got[k - 1]
     deg_i = jnp.sum(deg_i, axis=0, keepdims=True)
     scale_i = lax.rsqrt(jnp.maximum(deg_i, 1.0))
-    for k in (1, 3, 2):
-        arrive(dz_s + k, du_z.at[k - 1], z_dev(SIDE - k))
+    arrive(dz_s, du_z)
     deg_u = du_ysum[...] + du_z[0] + du_z[1] + du_z[2]
     scale_u = lax.rsqrt(jnp.maximum(deg_u, 1.0)).T
     for j in range(chunks):
@@ -323,26 +312,28 @@
         for h in range(tw // 128):
             sc_own[pl.ds(t * (tw // 128) + h, 1), :] = (pos - neg)[:, h * 128:(h + 1) * 128]
 
-    s_r, s_c = sems(rows), sems(chunks)
-    for k in ring:
-        push(s_r + k, sc_own, sc_row.at[k - 1], r_dev(k))
-    for k in ring:
-        arrive(s_r + k, sc_row.at[k - 1], r_dev(rows - k))
+    s_r, s_c = sems(1), sems(1)
+    for k in ring:
+        push(s_r, sc_own, sc_row.at[k - 1], r_dev(k))
+    arrive(s_r, sc_row)
     acc = sc_own[...]
     for k in ring:
         acc = acc + sc_row[k - 1]
     sc_sum[...] = acc
     for k in plane:
-        push(s_c + k, sc_sum, sc_col.at[k - 1], c_dev(k))
-    for k in plane:
-        arrive(s_c + k, sc_col.at[k - 1], c_dev(chunks - k))
+        push(s_c, sc_sum, sc_col.at[k - 1], c_dev(k))
+    arrive(s_c, sc_col)
     for k in plane:
         acc = acc + sc_col[k - 1]
     neg_x = -acc
     loss_ref[...] = jnp.maximum(neg_x, 0.0) + jnp.log1p(jnp.exp(-jnp.abs(neg_x)))
-    for one in sent:
-        one.wait_send()
-    assert count[0] <= send_sem.shape[0]
+    span = mask_buf.reshape(chunks * ublk, iblk)
+    whole = span.at[pl.ds(0, sum(sent) // (4 * iblk))]
+    copy(whole, whole, 0, {"row": r}).wait_send()
+    whole = i_nat.at[pl.ds(0, rows - 1)]
+    copy(whole, whole, 0, {"row": r}, 1).wait_send()
+    assert count[0] == recv_sem.shape[0]
+    assert sum(sent) % (32 * iblk) == 0
 
 
 def emit(ou_in, oi_in, loss_in, ou_ref, oi_ref, loss_ref):
@@ -364,7 +355,7 @@
         width = emb // rows
         tw = 256
         tiles = batch // tw
-        n_sem = 40 * (LAYERS + 1) + 32 * LAYERS + rows * (2 * LAYERS + 1) + 2 * SIDE + rows + rows + cols
+        n_sem = 10 * (LAYERS + 1) + 8 * LAYERS + 2 * LAYERS + 1 + 5
         vmem = pltpu.VMEM
         out_user, out_item, loss = pl.pallas_call(
             functools.partial(kernel, rows),
@@ -408,7 +399,7 @@
                 vmem((cols - 1, batch // 128, 128), F32),
                 vmem((rows, isub, emb), F32),
                 pltpu.SemaphoreType.DMA((cols,)),
-                pltpu.SemaphoreType.DMA((n_sem,)),
+                pltpu.SemaphoreType.DMA((2,)),
                 pltpu.SemaphoreType.DMA((n_sem,)),
             ],
             compiler_params=pltpu.CompilerParams(collective_id=0, has_side_effects=True),

time: 92.3 us -> 86.1 us (0.933)
  Pallas kernels: 91.4 us -> 85.2 us
    pallas_call x1, Pallas kernels: 90 us -> 83.8 us  [device_body(): pl.pallas_call(functools.partial(kernel, rows), name='lightgcn', out_shap...]
where the time goes in v3:
time: 86.1 us; the launch traced here: 85.8 us
  Pallas kernels  85.2 us (99%)
    pallas_call x1, Pallas kernels, device_body(): pl.pallas_call(functools.partial(kernel, rows), name='lightgcn', out_shap...  83.8 us

profile of v3, /device:TPU:1, one launch (start us, length us, event | category | flops | bytes accessed | tf_op | source)
XLA Modules:
  0.0 85.8 jit_solution(3611059164976182261)
XLA Ops:
  0.6 83.8 %lightgcn.1 = (bf16[64,256]{1,0:T(8,128)(2,1)}, bf16[64,64]{1,0:T(8,128)(2,1)}, f32[16,128]{1,0:T(8,128)}) custom-call(s32[4096,512]{1,0:T(8,128)} %mask_hbm.1, bf16[64,256]{1,0:T(8,128)(2,1)} %bitcast.4, bf16[64,64]{1,0:T(8,128)(2,1)} %ei_ref.1, s32[3,2048]{1,0:T(4,128)} %bitcast.5), custom_call_target="tpu_custom_call" | custom-call | tf_op jit(solution)/shard_map/lightgcn/pallas_call | solution.py:360
  84.4 1.4 %emit.1 = (bf16[64,256]{1,0:T(8,128)(2,1)}, bf16[64,64]{1,0:T(8,128)(2,1)}, f32[16,128]{1,0:T(8,128)}) custom-call(bf16[64,256]{1,0:T(8,128)(2,1)} %get-tuple-element.9.ou_in, bf16[64,64]{1,0:T(8,128)(2,1)} %get-tuple-element.10.oi_in, f32[16,128]{1,0:T(8,128)} %get-tuple-element.11.loss_in), custom_call_target="tpu_custom_call" | custom-call | tf_op jit(solution)/shard_map/emit/pallas_call | solution.py:407

commit v4 on v3

--- a/solution.py
+++ b/solution.py
@@ -30,7 +30,7 @@
 def kernel(
     rows, mask_hbm, eu_ref, ei_ref, tri_ref, ou_ref, oi_ref, loss_ref,
     mask_buf, adj, ua, ub, pa, pb, ra, rb, sa, sb, qa, qb, utot,
-    i_nat, i_pan, pi, ri, itot, du_own, du_y, du_ysum, du_z, di_own, di_got,
+    i_nat, i_pan, pi, ri, itot, du_own, du_y, du_ysum, du_z, du_inv, di_own, di_got,
     picks, sc_own, sc_row, sc_sum, sc_col, oi_nat,
     load_sem, send_sem, recv_sem,
 ):
@@ -99,8 +99,6 @@
     ua[0, y, z] = user0[:half]
     ub[0, z, y] = user0[half:]
     i_nat[r] = ei_ref[...]
-    pl.semaphore_wait(barrier, len(plane) + len(ring))
-
     ug = [sems(10) for _ in range(LAYERS + 1)]
 
     def user_gather_start(l):
@@ -127,20 +125,27 @@
 
     us = [sems(8) for _ in range(LAYERS)]
     groups = ((2, 2), (1, 1), (0, 1))
-
-    def user_product(l, panel):
-        def step(j, carry):
-            part = mm(panel, adj[j], NT)
-            jz, jy = lax.div(j, SIDE), lax.rem(j, SIDE)
-            pa[l, jy, plus(jz + SIDE, -z, SIDE)] = part[:half]
-            pb[l, jz, plus(jy + SIDE, -y, SIDE)] = part[half:]
-            return carry
-        lax.fori_loop(0, chunks, step, 0, unroll=4)
-        for g, (lo, n) in enumerate(groups):
-            for k in sides:
+    order = (
+        ((2, 2), (2, 3), (3, 2), (3, 3), (2, 1), (3, 1), (1, 2), (1, 3)),
+        ((1, 1),),
+        ((0, 1), (0, 2), (0, 3), (1, 0), (2, 0), (3, 0)),
+        ((0, 0),),
+    )
+
+    def user_product(l, panel, build=None):
+        for g, (lo, n) in enumerate(groups + ((0, 0),)):
+            for dz, dy in order[g]:
+                jz, jy = plus(z, dz, SIDE), plus(y, dy, SIDE)
+                j = jz * SIDE + jy
+                blk = adj[j] if build is None else build(j)
+                part = mm(panel, blk, NT)
+                pa[l, jy, dz] = part[:half]
+                pb[l, jz, dy] = part[half:]
+            if n:
                 part = pl.ds(lo, n)
-                push(us[l] + g, pa.at[l, plus(y, k, SIDE), part], ra.at[l, k - 1, part], y_dev(k))
-                push(us[l] + 4 + g, pb.at[l, plus(z, k, SIDE), part], rb.at[l, k - 1, part], z_dev(k))
+                for k in sides:
+                    push(us[l] + g, pa.at[l, plus(y, k, SIDE), part], ra.at[l, k - 1, part], y_dev(k))
+                    push(us[l] + 4 + g, pb.at[l, plus(z, k, SIDE), part], rb.at[l, k - 1, part], z_dev(k))
 
     def user_sum_1(l):
         for g, (lo, n) in enumerate(groups):
@@ -199,10 +204,6 @@
         arrive(ig[l], i_pan.at[l, pl.ds(0, rows - 1)])
         return i_pan[l].reshape(emb, iblk).astype(BF16)
 
-    user_gather_start(0)
-    for k in ring:
-        copy(i_nat.at[r], i_nat.at[r], ig[0], r_dev(k), 1).start()
-
     du_s, dz_s, di_s = sems(1), sems(1), sems(1)
     ones = jnp.ones((8, iblk), BF16)
     di_acc = jnp.zeros((8, iblk), jnp.int32)
@@ -214,20 +215,24 @@
         adj[j] = blk
         du_own[pl.ds(j, 1), :] = mm(ones, blk, NT)[:1]
     di_own[...] = di_acc.astype(F32)
+    pl.semaphore_wait(barrier, len(plane) + len(ring))
     for k in sides:
         push(du_s, du_own, du_y.at[k - 1], y_dev(k))
     for k in ring:
         push(di_s, di_own, di_got.at[k - 1], r_dev(k))
-    user_gather_fwd(0)
+    user_gather_start(0)
+    for k in ring:
+        copy(i_nat.at[r], i_nat.at[r], ig[0], r_dev(k), 1).start()
+    arrive(du_s, du_y)
+    du_ysum[...] = du_own[...] + du_y[0] + du_y[1] + du_y[2]
+    for k in sides:
+        push(dz_s, du_ysum, du_z.at[k - 1], z_dev(k))
     arrive(ig[0], i_nat.at[pl.ds(0, rows - 1)])
     item0 = mm(eye, i_nat[...].reshape(iblk, emb), NT)
     i_pan[0] = item0.reshape(i_pan.shape[1:])
     itot[...] = i_pan[0, r]
     item0 = item0.astype(BF16)
-    arrive(du_s, du_y)
-    du_ysum[...] = du_own[...] + du_y[0] + du_y[1] + du_y[2]
-    for k in sides:
-        push(dz_s, du_ysum, du_z.at[k - 1], z_dev(k))
+    user_gather_fwd(0)
     arrive(di_s, di_got)
     deg_i = di_own[...]
     for k in ring:
@@ -236,11 +241,15 @@
     scale_i = lax.rsqrt(jnp.maximum(deg_i, 1.0))
     arrive(dz_s, du_z)
     deg_u = du_ysum[...] + du_z[0] + du_z[1] + du_z[2]
-    scale_u = lax.rsqrt(jnp.maximum(deg_u, 1.0)).T
-    for j in range(chunks):
-        adj[j] = adj[j] * (scale_u[:, j:j + 1] * scale_i).astype(BF16)
-
-    user_product(0, item0)
+    du_inv[...] = lax.rsqrt(jnp.maximum(deg_u, 1.0))
+
+    def build(j):
+        scale_u = jnp.broadcast_to(du_inv[pl.ds(j, 1), :], (8, ublk)).T[:, :1]
+        blk = adj[j] * (scale_u * scale_i).astype(BF16)
+        adj[j] = blk
+        return blk
+
+    user_product(0, item0, build)
     user_gather_end(0)
     item_product(0)
     item_gather(1, item_sum(0))
@@ -390,6 +399,7 @@
                 vmem((3, cols, ublk), F32),
                 vmem((cols, ublk), F32),
                 vmem((3, cols, ublk), F32),
+                vmem((cols, ublk), F32),
                 vmem((8, iblk), F32),
                 vmem((rows - 1, 8, iblk), F32),
                 vmem((2, tiles, emb, tw), F32),

time: 86.1 us -> 84.7 us (0.984)
  Pallas kernels: 85.2 us -> 83.8 us
    pallas_call x1, Pallas kernels: 83.8 us -> 82.4 us  [device_body(): pl.pallas_call(functools.partial(kernel, rows), name='lightgcn', out_shap...]
where the time goes in v4:
time: 84.7 us; the launch traced here: 84.5 us
  Pallas kernels  83.8 us (99%)
    pallas_call x1, Pallas kernels, device_body(): pl.pallas_call(functools.partial(kernel, rows), name='lightgcn', out_shap...  82.4 us

profile of v4, /device:TPU:1, one launch (start us, length us, event | category | flops | bytes accessed | tf_op | source)
XLA Modules:
  0.0 84.5 jit_solution(4893056950267858693)
XLA Ops:
  0.6 82.4 %lightgcn.1 = (bf16[64,256]{1,0:T(8,128)(2,1)}, bf16[64,64]{1,0:T(8,128)(2,1)}, f32[16,128]{1,0:T(8,128)}) custom-call(s32[4096,512]{1,0:T(8,128)} %mask_hbm.1, bf16[64,256]{1,0:T(8,128)(2,1)} %bitcast.4, bf16[64,64]{1,0:T(8,128)(2,1)} %ei_ref.1, s32[3,2048]{1,0:T(4,128)} %bitcast.5), custom_call_target="tpu_custom_call" | custom-call | tf_op jit(solution)/shard_map/lightgcn/pallas_call | solution.py:369
  83.1 1.4 %emit.1 = (bf16[64,256]{1,0:T(8,128)(2,1)}, bf16[64,64]{1,0:T(8,128)(2,1)}, f32[16,128]{1,0:T(8,128)}) custom-call(bf16[64,256]{1,0:T(8,128)(2,1)} %get-tuple-element.9.ou_in, bf16[64,64]{1,0:T(8,128)(2,1)} %get-tuple-element.10.oi_in, f32[16,128]{1,0:T(8,128)} %get-tuple-element.11.loss_in), custom_call_target="tpu_custom_call" | custom-call | tf_op jit(solution)/shard_map/emit/pallas_call | solution.py:417

commit v5 on v4

--- a/solution.py
+++ b/solution.py
@@ -10,6 +10,7 @@
 
 LAYERS = 3
 SIDE = 4
+USER_SPAN = 128
 F32 = jnp.float32
 BF16 = jnp.bfloat16
 NN = (((1,), (0,)), ((), ()))
@@ -31,7 +32,8 @@
     rows, mask_hbm, eu_ref, ei_ref, tri_ref, ou_ref, oi_ref, loss_ref,
     mask_buf, adj, ua, ub, pa, pb, ra, rb, sa, sb, qa, qb, utot,
     i_nat, i_pan, pi, ri, itot, du_own, du_y, du_ysum, du_z, du_inv, di_own, di_got,
-    picks, sc_own, sc_row, sc_sum, sc_col, oi_nat,
+    oi_nat, oh, apick, ihit, ppa, ppb, pra, prb, psa, psb, pqa, pqb, upick,
+    vx, vxr, px, pxr, mrow, lcol,
     load_sem, send_sem, recv_sem,
 ):
     r = lax.axis_index("row")
@@ -43,7 +45,7 @@
     chunks = SIDE * SIDE
     iblk = adj.shape[-1]
     isub = i_nat.shape[1]
-    tiles, tw = picks.shape[1], picks.shape[3]
+    tiles, tw = apick.shape[:2]
 
     def plus(base, k, n):
         return lax.rem(base + k, n)
@@ -64,7 +66,7 @@
     plane = tuple(range(1, chunks))
     ring = tuple(range(1, rows))
     count = [0]
-    sent = []
+    sent, sent_small = [], []
 
     def sems(n):
         first = count[0]
@@ -77,8 +79,10 @@
             device_id=dev, device_id_type=pl.DeviceIdType.MESH)
 
     def push(sem, src, dst, dev):
-        copy(src, dst, sem, dev).start()
-        sent.append(math.prod(src.shape) * src.dtype.itemsize)
+        size = math.prod(src.shape) * src.dtype.itemsize
+        big = size % (32 * iblk) == 0
+        copy(src, dst, sem, dev, 0 if big else 2).start()
+        (sent if big else sent_small).append(size)
 
     def arrive(sem, whole):
         copy(whole, whole, sem, {"row": r}).wait_recv()
@@ -99,7 +103,7 @@
     ua[0, y, z] = user0[:half]
     ub[0, z, y] = user0[half:]
     i_nat[r] = ei_ref[...]
-    ug = [sems(10) for _ in range(LAYERS + 1)]
+    ug = [sems(10) for _ in range(LAYERS)]
 
     def user_gather_start(l):
         for k in sides:
@@ -123,7 +127,7 @@
         arrive(ug[l] + 8, ua.at[l, pl.ds(0, SIDE - 1)])
         arrive(ug[l] + 9, ub.at[l, pl.ds(0, SIDE - 1)])
 
-    us = [sems(8) for _ in range(LAYERS)]
+    us = [sems(8) for _ in range(LAYERS + 1)]
     groups = ((2, 2), (1, 1), (0, 1))
     order = (
         ((2, 2), (2, 3), (3, 2), (3, 3), (2, 1), (3, 1), (1, 2), (1, 3)),
@@ -132,8 +136,42 @@
         ((0, 0),),
     )
 
+    def layer_bufs(l):
+        return us[l], [ref.at[l] for ref in (pa, pb, ra, rb, sa, sb, qa, qb)]
+
+    pick_bufs = us[LAYERS], [ppa, ppb, pra, prb, psa, psb, pqa, pqb]
+
+    def sum_send(bufs, g):
+        sem, (own_a, own_b, got_a, got_b) = bufs[0], bufs[1][:4]
+        part = pl.ds(*groups[g])
+        for k in sides:
+            push(sem + g, own_a.at[plus(y, k, SIDE), part], got_a.at[k - 1, part], y_dev(k))
+            push(sem + 4 + g, own_b.at[plus(z, k, SIDE), part], got_b.at[k - 1, part], z_dev(k))
+
+    def sum_1(bufs):
+        sem, (own_a, own_b, got_a, got_b, mid_a, mid_b, end_a, end_b) = bufs
+        for g, (lo, n) in enumerate(groups):
+            part = pl.ds(lo, n)
+            arrive(sem + g, got_a.at[:, part])
+            arrive(sem + 4 + g, got_b.at[:, part])
+            for j in range(lo, lo + n):
+                mid_a[j] = own_a[y, j] + got_a[0, j] + got_a[1, j] + got_a[2, j]
+                mid_b[j] = own_b[z, j] + got_b[0, j] + got_b[1, j] + got_b[2, j]
+            for k in range(lo, lo + n):
+                if k:
+                    push(sem + 3, mid_a.at[k], end_a.at[k - 1], z_dev(k))
+                    push(sem + 7, mid_b.at[k], end_b.at[k - 1], y_dev(k))
+
+    def sum_2(bufs):
+        sem, (mid_a, mid_b, end_a, end_b) = bufs[0], bufs[1][4:]
+        arrive(sem + 3, end_a)
+        arrive(sem + 7, end_b)
+        next_a = (mid_a[0] + end_a[0] + end_a[1] + end_a[2]).astype(BF16)
+        next_b = (mid_b[0] + end_b[0] + end_b[1] + end_b[2]).astype(BF16)
+        return next_a, next_b
+
     def user_product(l, panel, build=None):
-        for g, (lo, n) in enumerate(groups + ((0, 0),)):
+        for g in range(len(order)):
             for dz, dy in order[g]:
                 jz, jy = plus(z, dz, SIDE), plus(y, dy, SIDE)
                 j = jz * SIDE + jy
@@ -141,30 +179,14 @@
                 part = mm(panel, blk, NT)
                 pa[l, jy, dz] = part[:half]
                 pb[l, jz, dy] = part[half:]
-            if n:
-                part = pl.ds(lo, n)
-                for k in sides:
-                    push(us[l] + g, pa.at[l, plus(y, k, SIDE), part], ra.at[l, k - 1, part], y_dev(k))
-                    push(us[l] + 4 + g, pb.at[l, plus(z, k, SIDE), part], rb.at[l, k - 1, part], z_dev(k))
+            if g < len(groups):
+                sum_send(layer_bufs(l), g)
 
     def user_sum_1(l):
-        for g, (lo, n) in enumerate(groups):
-            part = pl.ds(lo, n)
-            arrive(us[l] + g, ra.at[l, :, part])
-            arrive(us[l] + 4 + g, rb.at[l, :, part])
-            for j in range(lo, lo + n):
-                sa[l, j] = pa[l, y, j] + ra[l, 0, j] + ra[l, 1, j] + ra[l, 2, j]
-                sb[l, j] = pb[l, z, j] + rb[l, 0, j] + rb[l, 1, j] + rb[l, 2, j]
-            for k in range(lo, lo + n):
-                if k:
-                    push(us[l] + 3, sa.at[l, k], qa.at[l, k - 1], z_dev(k))
-                    push(us[l] + 7, sb.at[l, k], qb.at[l, k - 1], y_dev(k))
+        sum_1(layer_bufs(l))
 
     def user_sum_2(l):
-        arrive(us[l] + 3, qa.at[l])
-        arrive(us[l] + 7, qb.at[l])
-        next_a = (sa[l, 0] + qa[l, 0] + qa[l, 1] + qa[l, 2]).astype(BF16)
-        next_b = (sb[l, 0] + qb[l, 0] + qb[l, 1] + qb[l, 2]).astype(BF16)
+        next_a, next_b = sum_2(layer_bufs(l))
         utot[pl.ds(0, half)] += next_a.astype(F32)
         utot[pl.ds(half, half)] += next_b.astype(F32)
         return next_a, next_b
@@ -203,6 +225,70 @@
     def item_panel(l):
         arrive(ig[l], i_pan.at[l, pl.ds(0, rows - 1)])
         return i_pan[l].reshape(emb, iblk).astype(BF16)
+
+    def pick_rows(t):
+        ids = (tri_ref[0:1, t * tw:(t + 1) * tw] - r * (chunks * ublk)).astype(F32)
+        ids = jnp.broadcast_to(ids, (8, tw)).T[:, :1]
+        lane = lax.broadcasted_iota(jnp.int32, (tw, ublk), 1).astype(F32)
+        for j in range(chunks):
+            oh[:, j * ublk:(j + 1) * ublk] = jnp.where(ids - j * ublk == lane, 1.0, 0.0).astype(BF16)
+        rows_got = mm(oh[...], adj[...].reshape(chunks * ublk, iblk))
+        apick[t] = rows_got.astype(BF16)
+
+    def pick_product(panel):
+        for t in range(tiles):
+            part = mm(panel, apick[t], NT)
+            for h in range(tw // 128):
+                jz, jy = divmod(t * (tw // 128) + h, SIDE)
+                cut = part[:, h * 128:(h + 1) * 128]
+                ppa[jy, plus(jz + SIDE, -z, SIDE)] = cut[:half]
+                ppb[jz, plus(jy + SIDE, -y, SIDE)] = cut[half:]
+        for g in range(len(groups)):
+            sum_send(pick_bufs, g)
+
+    def pick_users(l):
+        local = tri_ref[0:1, pl.ds(pl.multiple_of(c * 128, 128), 128)] - r * (chunks * ublk)
+        blk_id = jnp.where(local < 0, -1, lax.div(local, ublk))
+        at_row = lax.broadcasted_iota(jnp.int32, (ublk, 128), 0)
+        hit = jnp.where(local - blk_id * ublk == at_row, 1.0, 0.0).astype(BF16)
+        got_a = mm(ua[l].reshape(chunks * half, ublk), hit)
+        got_b = mm(ub[l].reshape(chunks * half, ublk), hit)
+        vec_a = jnp.zeros((half, 128), F32)
+        vec_b = jnp.zeros((half, 128), F32)
+        for jz in range(SIDE):
+            for jy in range(SIDE):
+                here = blk_id == jz * SIDE + jy
+                ja = (jy * SIDE + jz) * half
+                jb = (jz * SIDE + jy) * half
+                vec_a = vec_a + jnp.where(here, got_a[ja:ja + half], 0.0)
+                vec_b = vec_b + jnp.where(here, got_b[jb:jb + half], 0.0)
+        if l:
+            vec_a = upick[pl.ds(0, half)] + vec_a
+            vec_b = upick[pl.ds(half, half)] + vec_b
+        upick[pl.ds(0, half)] = vec_a
+        upick[pl.ds(half, half)] = vec_b
+
+    def item_hits():
+        at_row = lax.broadcasted_iota(jnp.int32, (ublk, tw), 0)
+        for which in (1, 2):
+            for t in range(tiles):
+                local = tri_ref[which:which + 1, t * tw:(t + 1) * tw] - c * iblk
+                hit = lax.rem(local + USER_SPAN * ublk, ublk) == at_row
+                ihit[which - 1, t] = jnp.where(hit, 1.0, 0.0).astype(BF16)
+
+    def pick_items(mine):
+        lhs = jnp.concatenate([mine[:, h * ublk:(h + 1) * ublk] for h in range(iblk // ublk)], axis=0).astype(BF16)
+        width = mine.shape[0]
+        for which in (1, 2):
+            for t in range(tiles):
+                local = tri_ref[which:which + 1, t * tw:(t + 1) * tw] - c * iblk
+                got = mm(lhs, ihit[which - 1, t])
+                vec = jnp.zeros((width, tw), F32)
+                for h in range(iblk // ublk):
+                    here = (local >= h * ublk) & (local < (h + 1) * ublk)
+                    vec = vec + jnp.where(here, got[h * width:(h + 1) * width], 0.0)
+                for h in range(tw // 128):
+                    px[t * (tw // 128) + h, which - 1] = vec[:, h * 128:(h + 1) * 128]
 
     du_s, dz_s, di_s = sems(1), sems(1), sems(1)
     ones = jnp.ones((8, iblk), BF16)
@@ -249,100 +335,94 @@
         adj[j] = blk
         return blk
 
+    s_u, s_i, s_m, s_l = sems(1), sems(1), sems(1), sems(1)
     user_product(0, item0, build)
     user_gather_end(0)
     item_product(0)
+    pick_rows(0)
+    pick_rows(1)
+    pick_rows(2)
     item_gather(1, item_sum(0))
     user_sum_1(0)
     user_keep(1, *user_sum_2(0))
     user_gather_start(1)
+    pick_rows(3)
+    pick_rows(4)
     user_gather_fwd(1)
     user_product(1, item_panel(1))
+    pick_rows(5)
+    pick_rows(6)
+    pick_rows(7)
     user_gather_end(1)
     item_product(1)
+    item_hits()
+    pick_users(0)
+    pick_users(1)
     item_gather(2, item_sum(1))
     user_sum_1(1)
     user_keep(2, *user_sum_2(1))
     user_gather_start(2)
-    user_product(2, item_panel(2))
+    panel2 = item_panel(2)
+    pick_product(panel2)
     user_gather_fwd(2)
-    user_sum_1(2)
+    sum_1(pick_bufs)
+    user_product(2, panel2)
     user_gather_end(2)
     item_product(2)
+    pick_users(2)
+
+    vec_a, vec_b = sum_2(pick_bufs)
+    vec_a = ((upick[pl.ds(0, half)] + vec_a.astype(F32)) / (LAYERS + 1)).astype(BF16).astype(F32)
+    vec_b = ((upick[pl.ds(half, half)] + vec_b.astype(F32)) / (LAYERS + 1)).astype(BF16).astype(F32)
+    vx[...] = jnp.concatenate([vec_a, vec_b], axis=0).reshape(vx.shape)
+    for k in ring:
+        push(s_u, vx.at[plus(r, k, rows)], vxr.at[k - 1], r_dev(k))
+
+    item_sum(2)
+    out_slice = (itot[...] / (LAYERS + 1)).astype(BF16).astype(F32)
+    pick_items(out_slice)
+    for k in plane:
+        push(s_i, px.at[plus(c, k, chunks)], pxr.at[k - 1], c_dev(k))
+    item_gather(3, out_slice)
+    arrive(s_u, vxr)
+    vec_u = vx[r]
+    for k in ring:
+        vec_u = vec_u + vxr[k - 1]
+    user_sum_1(2)
+    arrive(s_i, pxr)
+    vec_p, vec_n = px[c, 0], px[c, 1]
+    for k in plane:
+        vec_p = vec_p + pxr[k - 1, 0]
+        vec_n = vec_n + pxr[k - 1, 1]
+    part = jnp.sum(vec_u * vec_p, axis=0, keepdims=True) - jnp.sum(vec_u * vec_n, axis=0, keepdims=True)
+    mrow[r] = jnp.broadcast_to(part, mrow.shape[1:])
+    for k in ring:
+        push(s_m, mrow.at[r], mrow.at[r], r_dev(k))
     user_sum_2(2)
-    out_ut = (utot[...] / (LAYERS + 1)).astype(BF16)
-    user_keep(3, out_ut[:half], out_ut[half:])
-    user_gather_start(3)
-    item_sum(2)
-    item_gather(3, (itot[...] / (LAYERS + 1)).astype(BF16).astype(F32))
-    ou_ref[...] = out_ut
-    user_gather_fwd(3)
-
+    ou_ref[...] = (utot[...] / (LAYERS + 1)).astype(BF16)
+    arrive(s_m, mrow.at[pl.ds(0, rows - 1)])
+    acc = mrow[0]
+    for k in range(1, rows):
+        acc = acc + mrow[k]
+    neg_x = -acc
+    lcol[c] = jnp.maximum(neg_x, 0.0) + jnp.log1p(jnp.exp(-jnp.abs(neg_x)))
+    for k in plane:
+        push(s_l, lcol.at[c], lcol.at[c], c_dev(k))
     out_it = item_panel(3)
     oi_nat[...] = mm(out_it, eye, TN).reshape(oi_nat.shape)
     oi_ref[...] = oi_nat[r].astype(BF16)
-    lane = ublk
-    at_row = lax.broadcasted_iota(jnp.int32, (lane, tw), 0)
-
-    def pick_items(which, t):
-        local = tri_ref[which:which + 1, t * tw:(t + 1) * tw] - c * iblk
-        got = jnp.zeros((emb, tw), F32)
-        for h in range(iblk // lane):
-            hit = jnp.where(local - h * lane == at_row, 1.0, 0.0).astype(BF16)
-            got = got + mm(out_it[:, h * lane:(h + 1) * lane], hit)
-        return got
-
-    for t in range(tiles):
-        picks[0, t] = pick_items(1, t)
-        picks[1, t] = pick_items(2, t)
-
-    user_gather_end(3)
-    stack_a = ua[3].reshape(chunks * half, ublk)
-    stack_b = ub[3].reshape(chunks * half, ublk)
-    for t in range(tiles):
-        local = tri_ref[0:1, t * tw:(t + 1) * tw] - r * (chunks * ublk)
-        blk_id = lax.div(local, ublk)
-        blk_id = jnp.where(local < 0, -1, blk_id)
-        hit = jnp.where(local - blk_id * ublk == at_row, 1.0, 0.0).astype(BF16)
-        got_a = mm(stack_a, hit)
-        got_b = mm(stack_b, hit)
-        vec_a = jnp.zeros((half, tw), F32)
-        vec_b = jnp.zeros((half, tw), F32)
-        for jz in range(SIDE):
-            for jy in range(SIDE):
-                here = blk_id == jz * SIDE + jy
-                ja = (jy * SIDE + jz) * half
-                jb = (jz * SIDE + jy) * half
-                vec_a = vec_a + jnp.where(here, got_a[ja:ja + half], 0.0)
-                vec_b = vec_b + jnp.where(here, got_b[jb:jb + half], 0.0)
-        vec = jnp.concatenate([vec_a, vec_b], axis=0)
-        pos = jnp.sum(vec * picks[0, t], axis=0, keepdims=True)
-        neg = jnp.sum(vec * picks[1, t], axis=0, keepdims=True)
-        for h in range(tw // 128):
-            sc_own[pl.ds(t * (tw // 128) + h, 1), :] = (pos - neg)[:, h * 128:(h + 1) * 128]
-
-    s_r, s_c = sems(1), sems(1)
-    for k in ring:
-        push(s_r, sc_own, sc_row.at[k - 1], r_dev(k))
-    arrive(s_r, sc_row)
-    acc = sc_own[...]
-    for k in ring:
-        acc = acc + sc_row[k - 1]
-    sc_sum[...] = acc
-    for k in plane:
-        push(s_c, sc_sum, sc_col.at[k - 1], c_dev(k))
-    arrive(s_c, sc_col)
-    for k in plane:
-        acc = acc + sc_col[k - 1]
-    neg_x = -acc
-    loss_ref[...] = jnp.maximum(neg_x, 0.0) + jnp.log1p(jnp.exp(-jnp.abs(neg_x)))
+    arrive(s_l, lcol.at[pl.ds(0, chunks - 1)])
+    loss_ref[...] = lcol[:, 0]
+
     span = mask_buf.reshape(chunks * ublk, iblk)
     whole = span.at[pl.ds(0, sum(sent) // (4 * iblk))]
     copy(whole, whole, 0, {"row": r}).wait_send()
+    whole = span.at[pl.ds(0, sum(sent_small) // 512), pl.ds(0, 128)]
+    copy(whole, whole, 0, {"row": r}, 2).wait_send()
     whole = i_nat.at[pl.ds(0, rows - 1)]
     copy(whole, whole, 0, {"row": r}, 1).wait_send()
     assert count[0] == recv_sem.shape[0]
-    assert sum(sent) % (32 * iblk) == 0
+    assert sum(sent_small) % 4096 == 0
 
 
 def emit(ou_in, oi_in, loss_in, ou_ref, oi_ref, loss_ref):
@@ -364,7 +444,7 @@
         width = emb // rows
         tw = 256
         tiles = batch // tw
-        n_sem = 10 * (LAYERS + 1) + 8 * LAYERS + 2 * LAYERS + 1 + 5
+        n_sem = 10 * LAYERS + 8 * (LAYERS + 1) + 2 * LAYERS + 1 + 3 + 4
         vmem = pltpu.VMEM
         out_user, out_item, loss = pl.pallas_call(
             functools.partial(kernel, rows),
@@ -379,8 +459,8 @@
             scratch_shapes=[
                 vmem((cols, ublk, iblk), jnp.int32),
                 vmem((cols, ublk, iblk), BF16),
-                vmem((LAYERS + 1, SIDE, SIDE, half, ublk), BF16),
-                vmem((LAYERS + 1, SIDE, SIDE, half, ublk), BF16),
+                vmem((LAYERS, SIDE, SIDE, half, ublk), BF16),
+                vmem((LAYERS, SIDE, SIDE, half, ublk), BF16),
                 vmem((LAYERS, SIDE, SIDE, half, ublk), F32),
                 vmem((LAYERS, SIDE, SIDE, half, ublk), F32),
                 vmem((LAYERS, 3, SIDE, half, ublk), F32),
@@ -402,14 +482,27 @@
                 vmem((cols, ublk), F32),
                 vmem((8, iblk), F32),
                 vmem((rows - 1, 8, iblk), F32),
-                vmem((2, tiles, emb, tw), F32),
-                vmem((batch // 128, 128), F32),
-                vmem((rows - 1, batch // 128, 128), F32),
-                vmem((batch // 128, 128), F32),
-                vmem((cols - 1, batch // 128, 128), F32),
                 vmem((rows, isub, emb), F32),
+                vmem((tw, cols * ublk), BF16),
+                vmem((tiles, tw, iblk), BF16),
+                vmem((2, tiles, ublk, tw), BF16),
+                vmem((SIDE, SIDE, half, 128), F32),
+                vmem((SIDE, SIDE, half, 128), F32),
+                vmem((3, SIDE, half, 128), F32),
+                vmem((3, SIDE, half, 128), F32),
+                vmem((SIDE, half, 128), F32),
+                vmem((SIDE, half, 128), F32),
+                vmem((3, half, 128), F32),
+                vmem((3, half, 128), F32),
+                vmem((emb, 128), F32),
+                vmem((rows, width, 128), F32),
+                vmem((rows - 1, width, 128), F32),
+                vmem((cols, 2, width, 128), F32),
+                vmem((cols - 1, 2, width, 128), F32),
+                vmem((rows, 8, 128), F32),
+                vmem((cols, 8, 128), F32),
                 pltpu.SemaphoreType.DMA((cols,)),
-                pltpu.SemaphoreType.DMA((2,)),
+                pltpu.SemaphoreType.DMA((3,)),
                 pltpu.SemaphoreType.DMA((n_sem,)),
             ],
             compiler_params=pltpu.CompilerParams(collective_id=0, has_side_effects=True),

time: 84.7 us -> 81.6 us (0.963)
  Pallas kernels: 83.8 us -> 80.7 us
    pallas_call x1, Pallas kernels: 82.4 us -> 79.3 us  [device_body(): pl.pallas_call(functools.partial(kernel, rows), name='lightgcn', out_shap...]
where the time goes in v5:
time: 81.6 us; the launch traced here: 81.4 us
  Pallas kernels  80.7 us (99%)
    pallas_call x1, Pallas kernels, device_body(): pl.pallas_call(functools.partial(kernel, rows), name='lightgcn', out_shap...  79.3 us

profile of v5, /device:TPU:1, one launch (start us, length us, event | category | flops | bytes accessed | tf_op | source)
XLA Modules:
  0.0 81.4 jit_solution(10523019451558347127)
XLA Ops:
  0.6 79.3 %lightgcn.1 = (bf16[64,256]{1,0:T(8,128)(2,1)}, bf16[64,64]{1,0:T(8,128)(2,1)}, f32[16,128]{1,0:T(8,128)}) custom-call(s32[4096,512]{1,0:T(8,128)} %mask_hbm.1, bf16[64,256]{1,0:T(8,128)(2,1)} %bitcast.4, bf16[64,64]{1,0:T(8,128)(2,1)} %ei_ref.1, s32[3,2048]{1,0:T(4,128)} %bitcast.5), custom_call_target="tpu_custom_call" | custom-call | tf_op jit(solution)/shard_map/lightgcn/pallas_call | solution.py:449
  80.0 1.4 %emit.1 = (bf16[64,256]{1,0:T(8,128)(2,1)}, bf16[64,64]{1,0:T(8,128)(2,1)}, f32[16,128]{1,0:T(8,128)}) custom-call(bf16[64,256]{1,0:T(8,128)(2,1)} %get-tuple-element.9.ou_in, bf16[64,64]{1,0:T(8,128)(2,1)} %get-tuple-element.10.oi_in, f32[16,128]{1,0:T(8,128)} %get-tuple-element.11.loss_in), custom_call_target="tpu_custom_call" | custom-call | tf_op jit(solution)/shard_map/emit/pallas_call | solution.py:510

commit v6 on v5

--- a/solution.py
+++ b/solution.py
@@ -33,7 +33,7 @@
     mask_buf, adj, ua, ub, pa, pb, ra, rb, sa, sb, qa, qb, utot,
     i_nat, i_pan, pi, ri, itot, du_own, du_y, du_ysum, du_z, du_inv, di_own, di_got,
     oi_nat, oh, apick, ihit, ppa, ppb, pra, prb, psa, psb, pqa, pqb, upick,
-    vx, vxr, px, pxr, mrow, lcol,
+    vx, vxr, px, pxr, tiny,
     load_sem, send_sem, recv_sem,
 ):
     r = lax.axis_index("row")
@@ -66,7 +66,7 @@
     plane = tuple(range(1, chunks))
     ring = tuple(range(1, rows))
     count = [0]
-    sent, sent_small = [], []
+    sent = [], [], []
 
     def sems(n):
         first = count[0]
@@ -80,9 +80,9 @@
 
     def push(sem, src, dst, dev):
         size = math.prod(src.shape) * src.dtype.itemsize
-        big = size % (32 * iblk) == 0
-        copy(src, dst, sem, dev, 0 if big else 2).start()
-        (sent if big else sent_small).append(size)
+        kind = 0 if size % (32 * iblk) == 0 else 1 if size % 4096 == 0 else 2
+        copy(src, dst, sem, dev, kind).start()
+        sent[kind].append(size)
 
     def arrive(sem, whole):
         copy(whole, whole, sem, {"row": r}).wait_recv()
@@ -170,17 +170,17 @@
         next_b = (mid_b[0] + end_b[0] + end_b[1] + end_b[2]).astype(BF16)
         return next_a, next_b
 
-    def user_product(l, panel, build=None):
-        for g in range(len(order)):
-            for dz, dy in order[g]:
-                jz, jy = plus(z, dz, SIDE), plus(y, dy, SIDE)
-                j = jz * SIDE + jy
-                blk = adj[j] if build is None else build(j)
-                part = mm(panel, blk, NT)
-                pa[l, jy, dz] = part[:half]
-                pb[l, jz, dy] = part[half:]
-            if g < len(groups):
-                sum_send(layer_bufs(l), g)
+    def user_product(l, panel, g, build=None):
+        for dz, dy in order[g]:
+            jz, jy = plus(z, dz, SIDE), plus(y, dy, SIDE)
+            j = jz * SIDE + jy
+            blk = adj[j] if build is None else build(j)
+            part = mm(panel, blk, NT)
+            pa[l, jy, dz] = part[:half]
+            pb[l, jz, dy] = part[half:]
+
+    def user_sum_send(l, g):
+        sum_send(layer_bufs(l), g)
 
     def user_sum_1(l):
         sum_1(layer_bufs(l))
@@ -308,7 +308,7 @@
         push(di_s, di_own, di_got.at[k - 1], r_dev(k))
     user_gather_start(0)
     for k in ring:
-        copy(i_nat.at[r], i_nat.at[r], ig[0], r_dev(k), 1).start()
+        copy(i_nat.at[r], i_nat.at[r], ig[0], r_dev(k), 3).start()
     arrive(du_s, du_y)
     du_ysum[...] = du_own[...] + du_y[0] + du_y[1] + du_y[2]
     for k in sides:
@@ -336,93 +336,114 @@
         return blk
 
     s_u, s_i, s_m, s_l = sems(1), sems(1), sems(1), sems(1)
-    user_product(0, item0, build)
+    user_product(0, item0, 0, build)
+    user_sum_send(0, 0)
+    user_product(0, item0, 1, build)
+    user_sum_send(0, 1)
+    user_product(0, item0, 2, build)
+    user_sum_send(0, 2)
+    user_product(0, item0, 3, build)
     user_gather_end(0)
     item_product(0)
     pick_rows(0)
+    mine = item_sum(0)
+    item_gather(1, mine)
     pick_rows(1)
-    pick_rows(2)
-    item_gather(1, item_sum(0))
     user_sum_1(0)
+    panel1 = item_panel(1)
+    user_product(1, panel1, 0)
+    user_sum_send(1, 0)
+    user_product(1, panel1, 1)
+    user_product(1, panel1, 2)
+    user_product(1, panel1, 3)
     user_keep(1, *user_sum_2(0))
     user_gather_start(1)
+    user_sum_send(1, 1)
+    pick_rows(2)
+    user_gather_fwd(1)
+    user_sum_send(1, 2)
     pick_rows(3)
     pick_rows(4)
-    user_gather_fwd(1)
-    user_product(1, item_panel(1))
     pick_rows(5)
-    pick_rows(6)
-    pick_rows(7)
+    user_sum_1(1)
     user_gather_end(1)
     item_product(1)
     item_hits()
     pick_users(0)
     pick_users(1)
-    item_gather(2, item_sum(1))
-    user_sum_1(1)
     user_keep(2, *user_sum_2(1))
     user_gather_start(2)
+    mine = item_sum(1)
+    item_gather(2, mine)
+    user_gather_fwd(2)
+    pick_rows(6)
+    pick_rows(7)
     panel2 = item_panel(2)
     pick_product(panel2)
-    user_gather_fwd(2)
-    sum_1(pick_bufs)
-    user_product(2, panel2)
     user_gather_end(2)
     item_product(2)
     pick_users(2)
-
-    vec_a, vec_b = sum_2(pick_bufs)
-    vec_a = ((upick[pl.ds(0, half)] + vec_a.astype(F32)) / (LAYERS + 1)).astype(BF16).astype(F32)
-    vec_b = ((upick[pl.ds(half, half)] + vec_b.astype(F32)) / (LAYERS + 1)).astype(BF16).astype(F32)
-    vx[...] = jnp.concatenate([vec_a, vec_b], axis=0).reshape(vx.shape)
-    for k in ring:
-        push(s_u, vx.at[plus(r, k, rows)], vxr.at[k - 1], r_dev(k))
-
+    sum_1(pick_bufs)
     item_sum(2)
     out_slice = (itot[...] / (LAYERS + 1)).astype(BF16).astype(F32)
     pick_items(out_slice)
     for k in plane:
         push(s_i, px.at[plus(c, k, chunks)], pxr.at[k - 1], c_dev(k))
+    vec_a, vec_b = sum_2(pick_bufs)
+    vec_a = ((upick[pl.ds(0, half)] + vec_a.astype(F32)) / (LAYERS + 1)).astype(BF16).astype(F32)
+    vec_b = ((upick[pl.ds(half, half)] + vec_b.astype(F32)) / (LAYERS + 1)).astype(BF16).astype(F32)
+    vx[...] = jnp.concatenate([vec_a, vec_b], axis=0).reshape(vx.shape)
+    for k in ring:
+        push(s_u, vx.at[plus(r, k, rows)], vxr.at[k - 1], r_dev(k))
+    user_product(2, panel2, 0)
+    user_sum_send(2, 0)
+    user_product(2, panel2, 1)
+    user_sum_send(2, 1)
+    user_product(2, panel2, 2)
+    user_sum_send(2, 2)
+    user_product(2, panel2, 3)
     item_gather(3, out_slice)
     arrive(s_u, vxr)
     vec_u = vx[r]
     for k in ring:
         vec_u = vec_u + vxr[k - 1]
-    user_sum_1(2)
     arrive(s_i, pxr)
     vec_p, vec_n = px[c, 0], px[c, 1]
     for k in plane:
         vec_p = vec_p + pxr[k - 1, 0]
         vec_n = vec_n + pxr[k - 1, 1]
     part = jnp.sum(vec_u * vec_p, axis=0, keepdims=True) - jnp.sum(vec_u * vec_n, axis=0, keepdims=True)
-    mrow[r] = jnp.broadcast_to(part, mrow.shape[1:])
-    for k in ring:
-        push(s_m, mrow.at[r], mrow.at[r], r_dev(k))
+    tiny[chunks + r] = part
+    for k in ring:
+        push(s_m, tiny.at[chunks + r], tiny.at[chunks + r], r_dev(k))
+    arrive(s_m, tiny.at[pl.ds(chunks, rows - 1)])
+    neg_x = -tiny[chunks]
+    for k in range(1, rows):
+        neg_x = neg_x - tiny[chunks + k]
+    tiny[c] = jnp.maximum(neg_x, 0.0) + jnp.log1p(jnp.exp(-jnp.abs(neg_x)))
+    for k in plane:
+        push(s_l, tiny.at[c], tiny.at[c], c_dev(k))
+    user_sum_1(2)
     user_sum_2(2)
     ou_ref[...] = (utot[...] / (LAYERS + 1)).astype(BF16)
-    arrive(s_m, mrow.at[pl.ds(0, rows - 1)])
-    acc = mrow[0]
-    for k in range(1, rows):
-        acc = acc + mrow[k]
-    neg_x = -acc
-    lcol[c] = jnp.maximum(neg_x, 0.0) + jnp.log1p(jnp.exp(-jnp.abs(neg_x)))
-    for k in plane:
-        push(s_l, lcol.at[c], lcol.at[c], c_dev(k))
     out_it = item_panel(3)
     oi_nat[...] = mm(out_it, eye, TN).reshape(oi_nat.shape)
     oi_ref[...] = oi_nat[r].astype(BF16)
-    arrive(s_l, lcol.at[pl.ds(0, chunks - 1)])
-    loss_ref[...] = lcol[:, 0]
+    arrive(s_l, tiny.at[pl.ds(0, chunks - 1)])
+    for k in range(chunks):
+        loss_ref[pl.ds(k, 1), :] = tiny[k]
 
     span = mask_buf.reshape(chunks * ublk, iblk)
-    whole = span.at[pl.ds(0, sum(sent) // (4 * iblk))]
-    copy(whole, whole, 0, {"row": r}).wait_send()
-    whole = span.at[pl.ds(0, sum(sent_small) // 512), pl.ds(0, 128)]
-    copy(whole, whole, 0, {"row": r}, 2).wait_send()
-    whole = i_nat.at[pl.ds(0, rows - 1)]
-    copy(whole, whole, 0, {"row": r}, 1).wait_send()
+    ends = (
+        span.at[pl.ds(0, sum(sent[0]) // (4 * iblk))],
+        span.at[pl.ds(0, sum(sent[1]) // 512), pl.ds(0, 128)],
+        tiny.at[pl.ds(0, sum(sent[2]) // 512)],
+        i_nat.at[pl.ds(0, rows - 1)],
+    )
+    for kind, whole in enumerate(ends):
+        copy(whole, whole, 0, {"row": r}, kind).wait_send()
     assert count[0] == recv_sem.shape[0]
-    assert sum(sent_small) % 4096 == 0
+    assert all(size % 512 == 0 for size in sent[2])
 
 
 def emit(ou_in, oi_in, loss_in, ou_ref, oi_ref, loss_ref):
@@ -499,10 +520,9 @@
                 vmem((rows - 1, width, 128), F32),
                 vmem((cols, 2, width, 128), F32),
                 vmem((cols - 1, 2, width, 128), F32),
-                vmem((rows, 8, 128), F32),
-                vmem((cols, 8, 128), F32),
+                vmem((cols + rows, 1, 128), F32),
                 pltpu.SemaphoreType.DMA((cols,)),
-                pltpu.SemaphoreType.DMA((3,)),
+                pltpu.SemaphoreType.DMA((4,)),
                 pltpu.SemaphoreType.DMA((n_sem,)),
             ],
             compiler_params=pltpu.CompilerParams(collective_id=0, has_side_effects=True),

time: 81.6 us -> 78.8 us (0.966)
  Pallas kernels: 80.7 us -> 77.9 us
    pallas_call x1, Pallas kernels: 79.3 us -> 76.5 us  [device_body(): pl.pallas_call(functools.partial(kernel, rows), name='lightgcn', out_shap...]
where the time goes in v6:
time: 78.8 us; the launch traced here: 78.5 us
  Pallas kernels  77.9 us (99%)
    pallas_call x1, Pallas kernels, device_body(): pl.pallas_call(functools.partial(kernel, rows), name='lightgcn', out_shap...  76.5 us

profile of v6, /device:TPU:1, one launch (start us, length us, event | category | flops | bytes accessed | tf_op | source)
XLA Modules:
  0.0 78.5 jit_solution(1186247826448795196)
XLA Ops:
  0.6 76.5 %lightgcn.1 = (bf16[64,256]{1,0:T(8,128)(2,1)}, bf16[64,64]{1,0:T(8,128)(2,1)}, f32[16,128]{1,0:T(8,128)}) custom-call(s32[4096,512]{1,0:T(8,128)} %mask_hbm.1, bf16[64,256]{1,0:T(8,128)(2,1)} %bitcast.4, bf16[64,64]{1,0:T(8,128)(2,1)} %ei_ref.1, s32[3,2048]{1,0:T(4,128)} %bitcast.5), custom_call_target="tpu_custom_call" | custom-call | tf_op jit(solution)/shard_map/lightgcn/pallas_call | solution.py:470
  77.1 1.4 %emit.1 = (bf16[64,256]{1,0:T(8,128)(2,1)}, bf16[64,64]{1,0:T(8,128)(2,1)}, f32[16,128]{1,0:T(8,128)}) custom-call(bf16[64,256]{1,0:T(8,128)(2,1)} %get-tuple-element.9.ou_in, bf16[64,64]{1,0:T(8,128)(2,1)} %get-tuple-element.10.oi_in, f32[16,128]{1,0:T(8,128)} %get-tuple-element.11.loss_in), custom_call_target="tpu_custom_call" | custom-call | tf_op jit(solution)/shard_map/emit/pallas_call | solution.py:530

commit v7 on v6

--- a/solution.py
+++ b/solution.py
@@ -11,6 +11,7 @@
 LAYERS = 3
 SIDE = 4
 USER_SPAN = 128
+AHEAD = 5
 F32 = jnp.float32
 BF16 = jnp.bfloat16
 NN = (((1,), (0,)), ((), ()))
@@ -88,7 +89,7 @@
         copy(whole, whole, sem, {"row": r}).wait_recv()
 
     loads = [pltpu.make_async_copy(mask_hbm.at[pl.ds(j * ublk, ublk)], mask_buf.at[j], load_sem.at[j]) for j in range(chunks)]
-    for one in loads:
+    for one in loads[:AHEAD]:
         one.start()
 
     barrier = pltpu.get_barrier_semaphore()
@@ -295,6 +296,8 @@
     di_acc = jnp.zeros((8, iblk), jnp.int32)
     for j in range(chunks):
         loads[j].wait()
+        if j + AHEAD < chunks:
+            loads[j + AHEAD].start()
         blk = mask_buf[j]
         di_acc = di_acc + jnp.sum(blk.reshape(ublk // 8, 8, iblk), axis=0)
         blk = blk.astype(F32).astype(BF16)
@@ -475,7 +478,7 @@
                 jax.ShapeDtypeStruct((isub, emb), BF16),
                 jax.ShapeDtypeStruct((batch // 128, 128), F32),
             ),
-            in_specs=[pl.BlockSpec(memory_space=pl.ANY)] + [pl.BlockSpec(memory_space=vmem)] * 3,
+            in_specs=[pl.BlockSpec(memory_space=pltpu.HBM)] + [pl.BlockSpec(memory_space=vmem)] * 3,
             out_specs=tuple([pl.BlockSpec(memory_space=vmem)] * 3),
             scratch_shapes=[
                 vmem((cols, ublk, iblk), jnp.int32),
@@ -525,7 +528,7 @@
                 pltpu.SemaphoreType.DMA((4,)),
                 pltpu.SemaphoreType.DMA((n_sem,)),
             ],
-            compiler_params=pltpu.CompilerParams(collective_id=0, has_side_effects=True),
+            compiler_params=pltpu.CompilerParams(collective_id=0, has_side_effects=True, vmem_limit_bytes=48 * 2**20),
         )(mask_blk, user_shard.T, item_shard, triples.T)
         out_user, out_item, loss = pl.pallas_call(
             emit,
@@ -535,6 +538,7 @@
                 jax.ShapeDtypeStruct((isub, emb), BF16),
                 jax.ShapeDtypeStruct((batch // 128, 128), F32),
             ),
+            compiler_params=pltpu.CompilerParams(vmem_limit_bytes=2**20),
         )(out_user, out_item, loss)
         return out_user.T, out_item, loss.reshape(batch)
 

time: 78.8 us -> 78.9 us (level)
  local copies, waits for them, and re-layouts: 0 us -> 2.23 us
  Pallas kernels: 77.9 us -> 75.7 us
    unnamed x0 -> x6, local copies, waits for them, and re-layouts: none -> 2.23 us
    pallas_call x1, Pallas kernels: 76.5 us -> 75 us  [device_body(): pl.pallas_call(functools.partial(kernel, rows), name='lightgcn', out_shap...]
where the time goes in v7:
time: 78.9 us; the launch traced here: 78.6 us
  Pallas kernels  75.7 us (96%)
  local copies, waits for them, and re-layouts  2.23 us (3%)
    pallas_call x1, Pallas kernels, device_body(): pl.pallas_call(functools.partial(kernel, rows), name='lightgcn', out_shap...  75 us
    unnamed x6, local copies, waits for them, and re-layouts  2.23 us

profile of v7, /device:TPU:1, one launch (start us, length us, event | category | flops | bytes accessed | tf_op | source)
XLA Modules:
  0.0 78.6 jit_solution(12021010599910047675)
XLA Ops:
  0.6 0.0 copy-start
  0.6 0.7 copy-done
  1.4 0.0 copy-start.1
  1.4 0.8 copy-done.1
  2.1 0.0 copy-start.2
  2.2 0.7 copy-done.2
  2.9 75.0 %lightgcn.1 = (bf16[64,256]{1,0:T(8,128)(2,1)S(1)}, bf16[64,64]{1,0:T(8,128)(2,1)S(1)}, f32[16,128]{1,0:T(8,128)S(1)}) custom-call(s32[4096,512]{1,0:T(8,128)} %mask_hbm.1, bf16[64,256]{1,0:T(8,128)(2,1)S(1)} %bitcast.4, bf16[64,64]{1,0:T(8,128)(2,1)S(1)} %copy-done.2, s32[3,2048]{1,0:T(4,128)S(1)} %bitcast.5), custom_call_target="tpu_custom_call" | custom-call | tf_op jit(solution)/shard_map/lightgcn/pallas_call | solution.py:473
  77.9 0.6 emit.1
Async XLA Ops:
  0.6 0.8 copy-start
  1.4 0.8 copy-start.1
  2.1 0.7 copy-start.2

commit v8 on v7

--- a/solution.py
+++ b/solution.py
@@ -30,12 +30,12 @@
 
 
 def kernel(
-    rows, mask_hbm, eu_ref, ei_ref, tri_ref, ou_ref, oi_ref, loss_ref,
+    rows, mask_hbm, eu_hbm, ei_hbm, tri_hbm, ou_ref, oi_ref, loss_ref,
     mask_buf, adj, ua, ub, pa, pb, ra, rb, sa, sb, qa, qb, utot,
     i_nat, i_pan, pi, ri, itot, du_own, du_y, du_ysum, du_z, du_inv, di_own, di_got,
     oi_nat, oh, apick, ihit, ppa, ppb, pra, prb, psa, psb, pqa, pqb, upick,
     vx, vxr, px, pxr, tiny,
-    load_sem, send_sem, recv_sem,
+    tri_ref, load_sem, send_sem, recv_sem,
 ):
     r = lax.axis_index("row")
     c = lax.axis_index("col")
@@ -91,19 +91,23 @@
     loads = [pltpu.make_async_copy(mask_hbm.at[pl.ds(j * ublk, ublk)], mask_buf.at[j], load_sem.at[j]) for j in range(chunks)]
     for one in loads[:AHEAD]:
         one.start()
+    smalls = [
+        pltpu.make_async_copy(eu_hbm.at[pl.ds(0, half)], ua.at[0, y, z], load_sem.at[chunks]),
+        pltpu.make_async_copy(eu_hbm.at[pl.ds(half, half)], ub.at[0, z, y], load_sem.at[chunks + 1]),
+        pltpu.make_async_copy(ei_hbm, i_nat.at[r], load_sem.at[chunks + 2]),
+        pltpu.make_async_copy(tri_hbm, tri_ref, load_sem.at[chunks + 3]),
+    ]
+    for one in smalls:
+        one.start()
 
     barrier = pltpu.get_barrier_semaphore()
-    for k in plane:
-        pl.semaphore_signal(barrier, inc=1, device_id=c_dev(k), device_id_type=pl.DeviceIdType.MESH)
+    for k in sides:
+        pl.semaphore_signal(barrier, inc=1, device_id=y_dev(k), device_id_type=pl.DeviceIdType.MESH)
+        pl.semaphore_signal(barrier, inc=1, device_id=z_dev(k), device_id_type=pl.DeviceIdType.MESH)
     for k in ring:
         pl.semaphore_signal(barrier, inc=1, device_id=r_dev(k), device_id_type=pl.DeviceIdType.MESH)
 
     eye = identity(emb)
-    user0 = eu_ref[...]
-    utot[...] = user0.astype(F32)
-    ua[0, y, z] = user0[:half]
-    ub[0, z, y] = user0[half:]
-    i_nat[r] = ei_ref[...]
     ug = [sems(10) for _ in range(LAYERS)]
 
     def user_gather_start(l):
@@ -304,12 +308,16 @@
         adj[j] = blk
         du_own[pl.ds(j, 1), :] = mm(ones, blk, NT)[:1]
     di_own[...] = di_acc.astype(F32)
-    pl.semaphore_wait(barrier, len(plane) + len(ring))
+    for one in smalls:
+        one.wait()
+    pl.semaphore_wait(barrier, 2 * len(sides) + len(ring))
     for k in sides:
         push(du_s, du_own, du_y.at[k - 1], y_dev(k))
     for k in ring:
         push(di_s, di_own, di_got.at[k - 1], r_dev(k))
     user_gather_start(0)
+    utot[pl.ds(0, half)] = ua[0, y, z].astype(F32)
+    utot[pl.ds(half, half)] = ub[0, z, y].astype(F32)
     for k in ring:
         copy(i_nat.at[r], i_nat.at[r], ig[0], r_dev(k), 3).start()
     arrive(du_s, du_y)
@@ -478,7 +486,7 @@
                 jax.ShapeDtypeStruct((isub, emb), BF16),
                 jax.ShapeDtypeStruct((batch // 128, 128), F32),
             ),
-            in_specs=[pl.BlockSpec(memory_space=pltpu.HBM)] + [pl.BlockSpec(memory_space=vmem)] * 3,
+            in_specs=[pl.BlockSpec(memory_space=pl.ANY)] * 4,
             out_specs=tuple([pl.BlockSpec(memory_space=vmem)] * 3),
             scratch_shapes=[
                 vmem((cols, ublk, iblk), jnp.int32),
@@ -524,11 +532,12 @@
                 vmem((cols, 2, width, 128), F32),
                 vmem((cols - 1, 2, width, 128), F32),
                 vmem((cols + rows, 1, 128), F32),
-                pltpu.SemaphoreType.DMA((cols,)),
+                vmem((3, batch), jnp.int32),
+                pltpu.SemaphoreType.DMA((cols + 4,)),
                 pltpu.SemaphoreType.DMA((4,)),
                 pltpu.SemaphoreType.DMA((n_sem,)),
             ],
-            compiler_params=pltpu.CompilerParams(collective_id=0, has_side_effects=True, vmem_limit_bytes=48 * 2**20),
+            compiler_params=pltpu.CompilerParams(collective_id=0, has_side_effects=True),
         )(mask_blk, user_shard.T, item_shard, triples.T)
         out_user, out_item, loss = pl.pallas_call(
             emit,
@@ -538,7 +547,6 @@
                 jax.ShapeDtypeStruct((isub, emb), BF16),
                 jax.ShapeDtypeStruct((batch // 128, 128), F32),
             ),
-            compiler_params=pltpu.CompilerParams(vmem_limit_bytes=2**20),
         )(out_user, out_item, loss)
         return out_user.T, out_item, loss.reshape(batch)
 

time: 78.9 us -> 78 us (0.989)
  local copies, waits for them, and re-layouts: 2.23 us -> 0 us
  Pallas kernels: 75.7 us -> 77.1 us
    unnamed x6 -> x0, local copies, waits for them, and re-layouts: 2.23 us -> none
where the time goes in v8:
time: 78 us; the launch traced here: 77.7 us
  Pallas kernels  77.1 us (99%)
    pallas_call x1, Pallas kernels, device_body(): pl.pallas_call(functools.partial(kernel, rows), name='lightgcn', out_shap...  75.7 us

profile of v8, /device:TPU:1, one launch (start us, length us, event | category | flops | bytes accessed | tf_op | source)
XLA Modules:
  0.0 77.7 jit_solution(2463250105423387462)
XLA Ops:
  0.6 75.7 %lightgcn.1 = (bf16[64,256]{1,0:T(8,128)(2,1)}, bf16[64,64]{1,0:T(8,128)(2,1)}, f32[16,128]{1,0:T(8,128)}) custom-call(s32[4096,512]{1,0:T(8,128)} %mask_hbm.1, bf16[64,256]{1,0:T(8,128)(2,1)} %bitcast.4, bf16[64,64]{1,0:T(8,128)(2,1)} %ei_hbm.1, s32[3,2048]{1,0:T(4,128)} %bitcast.5), custom_call_target="tpu_custom_call" | custom-call | tf_op jit(solution)/shard_map/lightgcn/pallas_call | solution.py:481
  76.3 1.4 %emit.1 = (bf16[64,256]{1,0:T(8,128)(2,1)}, bf16[64,64]{1,0:T(8,128)(2,1)}, f32[16,128]{1,0:T(8,128)}) custom-call(bf16[64,256]{1,0:T(8,128)(2,1)} %get-tuple-element.9.ou_in, bf16[64,64]{1,0:T(8,128)(2,1)} %get-tuple-element.10.oi_in, f32[16,128]{1,0:T(8,128)} %get-tuple-element.11.loss_in), custom_call_target="tpu_custom_call" | custom-call | tf_op jit(solution)/shard_map/emit/pallas_call | solution.py:542

commit v9 on v8

--- a/solution.py
+++ b/solution.py
@@ -11,7 +11,7 @@
 LAYERS = 3
 SIDE = 4
 USER_SPAN = 128
-AHEAD = 5
+AHEAD = 8
 F32 = jnp.float32
 BF16 = jnp.bfloat16
 NN = (((1,), (0,)), ((), ()))
@@ -88,14 +88,14 @@
     def arrive(sem, whole):
         copy(whole, whole, sem, {"row": r}).wait_recv()
 
-    loads = [pltpu.make_async_copy(mask_hbm.at[pl.ds(j * ublk, ublk)], mask_buf.at[j], load_sem.at[j]) for j in range(chunks)]
+    loads = [pltpu.make_async_copy(mask_hbm.at[pl.ds(j * ublk, ublk)], mask_buf.at[j], load_sem.at[j % AHEAD]) for j in range(chunks)]
     for one in loads[:AHEAD]:
         one.start()
     smalls = [
-        pltpu.make_async_copy(eu_hbm.at[pl.ds(0, half)], ua.at[0, y, z], load_sem.at[chunks]),
-        pltpu.make_async_copy(eu_hbm.at[pl.ds(half, half)], ub.at[0, z, y], load_sem.at[chunks + 1]),
-        pltpu.make_async_copy(ei_hbm, i_nat.at[r], load_sem.at[chunks + 2]),
-        pltpu.make_async_copy(tri_hbm, tri_ref, load_sem.at[chunks + 3]),
+        pltpu.make_async_copy(eu_hbm.at[pl.ds(0, half)], ua.at[0, y, z], load_sem.at[AHEAD]),
+        pltpu.make_async_copy(eu_hbm.at[pl.ds(half, half)], ub.at[0, z, y], load_sem.at[AHEAD + 1]),
+        pltpu.make_async_copy(ei_hbm, i_nat.at[r], load_sem.at[AHEAD + 2]),
+        pltpu.make_async_copy(tri_hbm, tri_ref, load_sem.at[AHEAD + 3]),
     ]
     for one in smalls:
         one.start()
@@ -132,10 +132,11 @@
         arrive(ug[l] + 8, ua.at[l, pl.ds(0, SIDE - 1)])
         arrive(ug[l] + 9, ub.at[l, pl.ds(0, SIDE - 1)])
 
-    us = [sems(8) for _ in range(LAYERS + 1)]
-    groups = ((2, 2), (1, 1), (0, 1))
+    us = [sems(10) for _ in range(LAYERS + 1)]
+    groups = ((2, 1), (3, 1), (1, 1), (0, 1))
     order = (
-        ((2, 2), (2, 3), (3, 2), (3, 3), (2, 1), (3, 1), (1, 2), (1, 3)),
+        ((2, 2), (2, 3), (3, 2), (2, 1), (1, 2)),
+        ((3, 3), (3, 1), (1, 3)),
         ((1, 1),),
         ((0, 1), (0, 2), (0, 3), (1, 0), (2, 0), (3, 0)),
         ((0, 0),),
@@ -151,26 +152,26 @@
         part = pl.ds(*groups[g])
         for k in sides:
             push(sem + g, own_a.at[plus(y, k, SIDE), part], got_a.at[k - 1, part], y_dev(k))
-            push(sem + 4 + g, own_b.at[plus(z, k, SIDE), part], got_b.at[k - 1, part], z_dev(k))
+            push(sem + 5 + g, own_b.at[plus(z, k, SIDE), part], got_b.at[k - 1, part], z_dev(k))
 
     def sum_1(bufs):
         sem, (own_a, own_b, got_a, got_b, mid_a, mid_b, end_a, end_b) = bufs
         for g, (lo, n) in enumerate(groups):
             part = pl.ds(lo, n)
             arrive(sem + g, got_a.at[:, part])
-            arrive(sem + 4 + g, got_b.at[:, part])
+            arrive(sem + 5 + g, got_b.at[:, part])
             for j in range(lo, lo + n):
                 mid_a[j] = own_a[y, j] + got_a[0, j] + got_a[1, j] + got_a[2, j]
                 mid_b[j] = own_b[z, j] + got_b[0, j] + got_b[1, j] + got_b[2, j]
             for k in range(lo, lo + n):
                 if k:
-                    push(sem + 3, mid_a.at[k], end_a.at[k - 1], z_dev(k))
-                    push(sem + 7, mid_b.at[k], end_b.at[k - 1], y_dev(k))
+                    push(sem + 4, mid_a.at[k], end_a.at[k - 1], z_dev(k))
+                    push(sem + 9, mid_b.at[k], end_b.at[k - 1], y_dev(k))
 
     def sum_2(bufs):
         sem, (mid_a, mid_b, end_a, end_b) = bufs[0], bufs[1][4:]
-        arrive(sem + 3, end_a)
-        arrive(sem + 7, end_b)
+        arrive(sem + 4, end_a)
+        arrive(sem + 9, end_b)
         next_a = (mid_a[0] + end_a[0] + end_a[1] + end_a[2]).astype(BF16)
         next_b = (mid_b[0] + end_b[0] + end_b[1] + end_b[2]).astype(BF16)
         return next_a, next_b
@@ -354,6 +355,8 @@
     user_product(0, item0, 2, build)
     user_sum_send(0, 2)
     user_product(0, item0, 3, build)
+    user_sum_send(0, 3)
+    user_product(0, item0, 4, build)
     user_gather_end(0)
     item_product(0)
     pick_rows(0)
@@ -365,14 +368,16 @@
     user_product(1, panel1, 0)
     user_sum_send(1, 0)
     user_product(1, panel1, 1)
+    user_sum_send(1, 1)
     user_product(1, panel1, 2)
     user_product(1, panel1, 3)
+    user_product(1, panel1, 4)
     user_keep(1, *user_sum_2(0))
     user_gather_start(1)
-    user_sum_send(1, 1)
+    user_sum_send(1, 2)
     pick_rows(2)
     user_gather_fwd(1)
-    user_sum_send(1, 2)
+    user_sum_send(1, 3)
     pick_rows(3)
     pick_rows(4)
     pick_rows(5)
@@ -413,6 +418,8 @@
     user_product(2, panel2, 2)
     user_sum_send(2, 2)
     user_product(2, panel2, 3)
+    user_sum_send(2, 3)
+    user_product(2, panel2, 4)
     item_gather(3, out_slice)
     arrive(s_u, vxr)
     vec_u = vx[r]
@@ -476,7 +483,7 @@
         width = emb // rows
         tw = 256
         tiles = batch // tw
-        n_sem = 10 * LAYERS + 8 * (LAYERS + 1) + 2 * LAYERS + 1 + 3 + 4
+        n_sem = 10 * LAYERS + 10 * (LAYERS + 1) + 2 * LAYERS + 1 + 3 + 4
         vmem = pltpu.VMEM
         out_user, out_item, loss = pl.pallas_call(
             functools.partial(kernel, rows),
@@ -533,7 +540,7 @@
                 vmem((cols - 1, 2, width, 128), F32),
                 vmem((cols + rows, 1, 128), F32),
                 vmem((3, batch), jnp.int32),
-                pltpu.SemaphoreType.DMA((cols + 4,)),
+                pltpu.SemaphoreType.DMA((AHEAD + 4,)),
                 pltpu.SemaphoreType.DMA((4,)),
                 pltpu.SemaphoreType.DMA((n_sem,)),
             ],

time: 78 us -> 76.8 us (0.985)
  Pallas kernels: 77.1 us -> 75.9 us
    pallas_call x1, Pallas kernels: 75.7 us -> 74.5 us  [device_body(): pl.pallas_call(functools.partial(kernel, rows), name='lightgcn', out_shap...]
where the time goes in v9:
time: 76.8 us; the launch traced here: 76.6 us
  Pallas kernels  75.9 us (99%)
    pallas_call x1, Pallas kernels, device_body(): pl.pallas_call(functools.partial(kernel, rows), name='lightgcn', out_shap...  74.5 us

profile of v9, /device:TPU:1, one launch (start us, length us, event | category | flops | bytes accessed | tf_op | source)
XLA Modules:
  0.0 76.6 jit_solution(3019139647254174372)
XLA Ops:
  0.6 74.5 %lightgcn.1 = (bf16[64,256]{1,0:T(8,128)(2,1)}, bf16[64,64]{1,0:T(8,128)(2,1)}, f32[16,128]{1,0:T(8,128)}) custom-call(s32[4096,512]{1,0:T(8,128)} %mask_hbm.1, bf16[64,256]{1,0:T(8,128)(2,1)} %bitcast.4, bf16[64,64]{1,0:T(8,128)(2,1)} %ei_hbm.1, s32[3,2048]{1,0:T(4,128)} %bitcast.5), custom_call_target="tpu_custom_call" | custom-call | tf_op jit(solution)/shard_map/lightgcn/pallas_call | solution.py:488
  75.2 1.4 %emit.1 = (bf16[64,256]{1,0:T(8,128)(2,1)}, bf16[64,64]{1,0:T(8,128)(2,1)}, f32[16,128]{1,0:T(8,128)}) custom-call(bf16[64,256]{1,0:T(8,128)(2,1)} %get-tuple-element.9.ou_in, bf16[64,64]{1,0:T(8,128)(2,1)} %get-tuple-element.10.oi_in, f32[16,128]{1,0:T(8,128)} %get-tuple-element.11.loss_in), custom_call_target="tpu_custom_call" | custom-call | tf_op jit(solution)/shard_map/emit/pallas_call | solution.py:549

commit v10 on v9

--- a/solution.py
+++ b/solution.py
@@ -66,6 +66,8 @@
     sides = (2, 1, 3)
     plane = tuple(range(1, chunks))
     ring = tuple(range(1, rows))
+    far_ring = tuple(sorted(ring, key=lambda k: -min(k, rows - k)))
+    far_plane = tuple(sorted(plane, key=lambda k: -min(k % SIDE, SIDE - k % SIDE) - min(k // SIDE, SIDE - k // SIDE)))
     count = [0]
     sent = [], [], []
 
@@ -211,12 +213,12 @@
             return acc + mm(lhs, adj[j])
         acc = lax.fori_loop(0, chunks, step, jnp.zeros((emb, iblk), F32), unroll=4)
         pi[l] = acc.reshape(pi.shape[1:])
-        for k in ring:
+        for k in far_ring:
             push(isum[l], pi.at[l, plus(r, k, rows)], ri.at[l, k - 1], r_dev(k))
 
     def item_gather(l, mine):
         i_pan[l, r] = mine
-        for k in ring:
+        for k in far_ring:
             push(ig[l], i_pan.at[l, r], i_pan.at[l, r], r_dev(k))
 
     def item_sum(l):
@@ -314,12 +316,12 @@
     pl.semaphore_wait(barrier, 2 * len(sides) + len(ring))
     for k in sides:
         push(du_s, du_own, du_y.at[k - 1], y_dev(k))
-    for k in ring:
+    for k in far_ring:
         push(di_s, di_own, di_got.at[k - 1], r_dev(k))
     user_gather_start(0)
     utot[pl.ds(0, half)] = ua[0, y, z].astype(F32)
     utot[pl.ds(half, half)] = ub[0, z, y].astype(F32)
-    for k in ring:
+    for k in far_ring:
         copy(i_nat.at[r], i_nat.at[r], ig[0], r_dev(k), 3).start()
     arrive(du_s, du_y)
     du_ysum[...] = du_own[...] + du_y[0] + du_y[1] + du_y[2]
@@ -403,13 +405,13 @@
     item_sum(2)
     out_slice = (itot[...] / (LAYERS + 1)).astype(BF16).astype(F32)
     pick_items(out_slice)
-    for k in plane:
+    for k in far_plane:
         push(s_i, px.at[plus(c, k, chunks)], pxr.at[k - 1], c_dev(k))
     vec_a, vec_b = sum_2(pick_bufs)
     vec_a = ((upick[pl.ds(0, half)] + vec_a.astype(F32)) / (LAYERS + 1)).astype(BF16).astype(F32)
     vec_b = ((upick[pl.ds(half, half)] + vec_b.astype(F32)) / (LAYERS + 1)).astype(BF16).astype(F32)
     vx[...] = jnp.concatenate([vec_a, vec_b], axis=0).reshape(vx.shape)
-    for k in ring:
+    for k in far_ring:
         push(s_u, vx.at[plus(r, k, rows)], vxr.at[k - 1], r_dev(k))
     user_product(2, panel2, 0)
     user_sum_send(2, 0)
@@ -432,14 +434,14 @@
         vec_n = vec_n + pxr[k - 1, 1]
     part = jnp.sum(vec_u * vec_p, axis=0, keepdims=True) - jnp.sum(vec_u * vec_n, axis=0, keepdims=True)
     tiny[chunks + r] = part
-    for k in ring:
+    for k in far_ring:
         push(s_m, tiny.at[chunks + r], tiny.at[chunks + r], r_dev(k))
     arrive(s_m, tiny.at[pl.ds(chunks, rows - 1)])
     neg_x = -tiny[chunks]
     for k in range(1, rows):
         neg_x = neg_x - tiny[chunks + k]
     tiny[c] = jnp.maximum(neg_x, 0.0) + jnp.log1p(jnp.exp(-jnp.abs(neg_x)))
-    for k in plane:
+    for k in far_plane:
         push(s_l, tiny.at[c], tiny.at[c], c_dev(k))
     user_sum_1(2)
     user_sum_2(2)

time: 76.8 us -> 76.4 us (level)
  no operation moved by 1% of the time
where the time goes in v10:
time: 76.4 us; the launch traced here: 76.2 us
  Pallas kernels  75.6 us (99%)
    pallas_call x1, Pallas kernels, device_body(): pl.pallas_call(functools.partial(kernel, rows), name='lightgcn', out_shap...  74.2 us

profile of v10, /device:TPU:1, one launch (start us, length us, event | category | flops | bytes accessed | tf_op | source)
XLA Modules:
  0.0 76.2 jit_solution(606257784282215006)
XLA Ops:
  0.6 74.2 %lightgcn.1 = (bf16[64,256]{1,0:T(8,128)(2,1)}, bf16[64,64]{1,0:T(8,128)(2,1)}, f32[16,128]{1,0:T(8,128)}) custom-call(s32[4096,512]{1,0:T(8,128)} %mask_hbm.1, bf16[64,256]{1,0:T(8,128)(2,1)} %bitcast.4, bf16[64,64]{1,0:T(8,128)(2,1)} %ei_hbm.1, s32[3,2048]{1,0:T(4,128)} %bitcast.5), custom_call_target="tpu_custom_call" | custom-call | tf_op jit(solution)/shard_map/lightgcn/pallas_call | solution.py:490
  74.8 1.4 %emit.1 = (bf16[64,256]{1,0:T(8,128)(2,1)}, bf16[64,64]{1,0:T(8,128)(2,1)}, f32[16,128]{1,0:T(8,128)}) custom-call(bf16[64,256]{1,0:T(8,128)(2,1)} %get-tuple-element.9.ou_in, bf16[64,64]{1,0:T(8,128)(2,1)} %get-tuple-element.10.oi_in, f32[16,128]{1,0:T(8,128)} %get-tuple-element.11.loss_in), custom_call_target="tpu_custom_call" | custom-call | tf_op jit(solution)/shard_map/emit/pallas_call | solution.py:551

commit v11 on v10

--- a/solution.py
+++ b/solution.py
@@ -110,7 +110,8 @@
         pl.semaphore_signal(barrier, inc=1, device_id=r_dev(k), device_id_type=pl.DeviceIdType.MESH)
 
     eye = identity(emb)
-    ug = [sems(10) for _ in range(LAYERS)]
+    ug = [sems(10) for _ in range(2)]
+    ug.append(ug[0])
 
     def user_gather_start(l):
         for k in sides:
@@ -134,7 +135,8 @@
         arrive(ug[l] + 8, ua.at[l, pl.ds(0, SIDE - 1)])
         arrive(ug[l] + 9, ub.at[l, pl.ds(0, SIDE - 1)])
 
-    us = [sems(10) for _ in range(LAYERS + 1)]
+    us = [sems(10) for _ in range(2)]
+    us += [us[1], us[0]]
     groups = ((2, 1), (3, 1), (1, 1), (0, 1))
     order = (
         ((2, 2), (2, 3), (3, 2), (2, 1), (1, 2)),
@@ -485,7 +487,7 @@
         width = emb // rows
         tw = 256
         tiles = batch // tw
-        n_sem = 10 * LAYERS + 10 * (LAYERS + 1) + 2 * LAYERS + 1 + 3 + 4
+        n_sem = 20 + 20 + 2 * LAYERS + 1 + 3 + 4
         vmem = pltpu.VMEM
         out_user, out_item, loss = pl.pallas_call(
             functools.partial(kernel, rows),

time: 76.4 us -> 76.2 us (level)
  no operation moved by 1% of the time
where the time goes in v11:
time: 76.2 us; the launch traced here: 76 us
  Pallas kernels  75.3 us (99%)
    pallas_call x1, Pallas kernels, device_body(): pl.pallas_call(functools.partial(kernel, rows), name='lightgcn', out_shap...  73.9 us

profile of v11, /device:TPU:1, one launch (start us, length us, event | category | flops | bytes accessed | tf_op | source)
XLA Modules:
  0.0 76.0 jit_solution(9849776037065301784)
XLA Ops:
  0.6 73.9 %lightgcn.1 = (bf16[64,256]{1,0:T(8,128)(2,1)}, bf16[64,64]{1,0:T(8,128)(2,1)}, f32[16,128]{1,0:T(8,128)}) custom-call(s32[4096,512]{1,0:T(8,128)} %mask_hbm.1, bf16[64,256]{1,0:T(8,128)(2,1)} %bitcast.4, bf16[64,64]{1,0:T(8,128)(2,1)} %ei_hbm.1, s32[3,2048]{1,0:T(4,128)} %bitcast.5), custom_call_target="tpu_custom_call" | custom-call | tf_op jit(solution)/shard_map/lightgcn/pallas_call | solution.py:492
  74.6 1.4 %emit.1 = (bf16[64,256]{1,0:T(8,128)(2,1)}, bf16[64,64]{1,0:T(8,128)(2,1)}, f32[16,128]{1,0:T(8,128)}) custom-call(bf16[64,256]{1,0:T(8,128)(2,1)} %get-tuple-element.9.ou_in, bf16[64,64]{1,0:T(8,128)(2,1)} %get-tuple-element.10.oi_in, f32[16,128]{1,0:T(8,128)} %get-tuple-element.11.loss_in), custom_call_target="tpu_custom_call" | custom-call | tf_op jit(solution)/shard_map/emit/pallas_call | solution.py:553
